TPU v7x, 1024 devices: a whole 4x8x16 slice. The times are simulated.
1024 devices in a mesh: grp: 32 (over y_hi, z), shell: 32 (over x, y_lo, core).
Axes of the slice: x: 4, y: 8 (y_hi: 2, y_lo: 4; y = y_hi * 4 + y_lo), z: 16, core: 2. Of those that a mesh axis runs over, the one named last changes fastest.
Arguments:
- vectors: bfloat16 [32, 32, 384, 256], P('grp', 'shell'), may hold values from -6 to 6
- local_block: bfloat16 [32, 32, 384, 384], P('grp', 'shell'), may hold values from -0.3125 to 0.3125
- pair_blocks: bfloat16 [32, 32, 4, 384, 384], P('grp', 'shell'), may hold values from -0.3125 to 0.3125
- pair_masks: int32 [32, 32, 4, 3, 3], P('grp', 'shell'), may hold values 0 or 1
- shell_block: bfloat16 [32, 32, 384, 384], P('grp', 'shell'), may hold values from -0.3125 to 0.3125
- shell_mask: int32 [32, 32, 3, 3], P('grp', 'shell'), may hold values 0 or 1
- matchings: int32 [4, 32], replicated, may hold values from 0 to 31, as said below
Outputs:
- filtered: bfloat16 [32, 32, 384, 256], P('grp', 'shell')
Inputs may be any that keep to these rules, and one draw needn't show every extreme that they name: Row m of matchings maps every group g to g XOR 2**b_m, for 4 distinct binary digits b_m drawn from the seed.
All inputs are finite; a program needn't handle non-finite values. No bound on the sum of `pair_masks` or of `shell_mask` on one device may be relied on, other than what follows from the above.
Results may differ from a plain program's by a relative error of at most 0.0049.
Values may be sent and summed in bfloat16 or wider, within the bound.
No kernel may reach another device: no remote copies, remote signals or barrier semaphores. Data moves between devices by JAX's collectives and lax.ppermute only.
A program may use at most 32 MiB of HBM per device.

v0:
```python
import jax
import jax.numpy as jnp
from jax import lax
from jax.sharding import PartitionSpec as P

BLK = 128


spectrum_center = 1.0
spectrum_halfwidth = 6.0


def from_behind(block, axis, distance):
    devices = range(lax.axis_size(axis))
    route = [(i - distance, i) for i in devices if i - distance in devices]
    return lax.ppermute(block, axis, route)


def from_partner(x, axis, distance):
    return lax.ppermute(x, axis, [(i, i ^ 1 << distance) for i in range(lax.axis_size(axis))])


def widen(mask):
    spread = jnp.repeat(jnp.repeat(mask, BLK, axis=-2), BLK, axis=-1)
    return spread.astype(jnp.bfloat16)


def select_sum(arrays, switches):
    accumulated_rows = jnp.zeros_like(arrays[0])
    for member, switch in zip(arrays, switches):
        accumulated_rows = accumulated_rows + jnp.where(switch, member, jnp.zeros_like(member))
    return accumulated_rows


def transposed(block, current):
    return lax.dot_general(
        block, current, (((0,), (0,)), ((), ())), preferred_element_type=jnp.float32
    )


def on_device(vectors, local_block, pair_blocks, pair_masks, shell_block, shell_mask, matchings):
    initial = vectors[0, 0]
    owned_rows = local_block[0, 0]
    coupled_rows = pair_blocks[0, 0] * widen(pair_masks[0, 0])
    upper_block = shell_block[0, 0] * widen(shell_mask[0, 0])
    matching_total = coupled_rows.shape[0]
    bit_total = lax.axis_size("grp").bit_length() - 1
    group_index = lax.axis_index("grp")
    flip_bits = jnp.bitwise_xor(matchings[:, group_index], group_index)
    chosen = [
        [flip_bits[pairing_index] == 1 << bit_index for bit_index in range(bit_total)]
        for pairing_index in range(matching_total)
    ]

    def operate(current):
        accumulated_rows = jnp.dot(
            owned_rows, current, preferred_element_type=jnp.float32
        ) + transposed(owned_rows, current)
        higher_partner = from_behind(current, "shell", -1)
        accumulated_rows = accumulated_rows + jnp.dot(
            upper_block, higher_partner, preferred_element_type=jnp.float32
        )
        returned = jnp.einsum(
            "mkr,kv->mrv", coupled_rows, current, preferred_element_type=jnp.float32
        ).astype(jnp.bfloat16)
        payload = jnp.stack([jnp.broadcast_to(current, returned.shape), returned], axis=1)
        arrived = []
        for bit_index in range(bit_total):
            outgoing = select_sum(
                [payload[pairing_index] for pairing_index in range(matching_total)],
                [chosen[pairing_index][bit_index] for pairing_index in range(matching_total)],
            )
            arrived.append(from_partner(outgoing, "grp", bit_index))
        received = jnp.stack(
            [select_sum(arrived, chosen[pairing_index]) for pairing_index in range(matching_total)]
        )
        accumulated_rows = accumulated_rows + jnp.einsum(
            "mrk,mkv->rv", coupled_rows, received[:, 0], preferred_element_type=jnp.float32
        )
        accumulated_rows = accumulated_rows + jnp.sum(received[:, 1].astype(jnp.float32), axis=0)
        upward = transposed(upper_block, current).astype(jnp.bfloat16)
        accumulated_rows = accumulated_rows + from_behind(upward, "shell", 1).astype(jnp.float32)
        return accumulated_rows

    current = (
        (operate(initial) - spectrum_center * initial.astype(jnp.float32)) / spectrum_halfwidth
    ).astype(jnp.bfloat16)
    image = operate(current)
    following = 2.0 * (
        image - spectrum_center * current.astype(jnp.float32)
    ) / spectrum_halfwidth - initial.astype(jnp.float32)
    current = following.astype(jnp.bfloat16)
    return current[None, None]


def solution(mesh):
    in_specs = (
        P("grp", "shell", None, None),
        P("grp", "shell", None, None),
        P("grp", "shell", None, None, None),
        P("grp", "shell", None, None, None),
        P("grp", "shell", None, None),
        P("grp", "shell", None, None),
        P(),
    )
    out_specs = P("grp", "shell", None, None)
    return jax.shard_map(
        on_device, mesh=mesh, in_specs=in_specs, out_specs=out_specs, check_vma=False
    )
```

profile of v0, /device:TPU:129, one launch (start us, length us, event | category | flops | bytes accessed | tf_op | source)
XLA Modules:
  0.0 208.9 jit_solution(2349499240250736563)
XLA Ops:
  6.3 1.8 copy.47
  10.9 7.4 %collective-permute-start.5 = (bf16[2,384,256]{2,1,0:T(8,128)(2,1)}, bf16[2,384,256]{2,1,0:T(8,128)(2,1)S(1)}, u32[]{:S(2)}, u32[]{:S(2)}) collective-permute-start(bf16[2,384,256]{2,1,0:T(8,128)(2,1)} %fusion.29), channel_id=1, source_target_pairs={{0,512},{32,544},{64,576},{96,608},{128,640},{160,672},{192,704},{... | collective-permute-start | bytes 1179656 | tf_op jit(solution)/shard_map/ppermute | solution.py:20
  25.7 1.3 fusion.33
  27.0 17.4 %collective-permute-start.4 = (bf16[2,384,256]{2,1,0:T(8,128)(2,1)}, bf16[2,384,256]{2,1,0:T(8,128)(2,1)}, u32[]{:S(2)}, u32[]{:S(2)}) collective-permute-start(bf16[2,384,256]{2,1,0:T(8,128)(2,1)} %get-tuple-element.22), channel_id=1, source_target_pairs={{0,256},{32,288},{64,320},{96,352},{128,384},{160,416},{192,448},{... | collective-permute-start | bytes 1179656 | tf_op jit(solution)/shard_map/ppermute | solution.py:20
  44.4 5.8 %collective-permute-start.3 = (bf16[2,384,256]{2,1,0:T(8,128)(2,1)}, bf16[2,384,256]{2,1,0:T(8,128)(2,1)}, u32[]{:S(2)}, u32[]{:S(2)}) collective-permute-start(bf16[2,384,256]{2,1,0:T(8,128)(2,1)} %get-tuple-element.21), channel_id=1, source_target_pairs={{0,128},{32,160},{64,192},{96,224},{128,0},{160,32},{192,64},{224,... | collective-permute-start | bytes 1179656 | tf_op jit(solution)/shard_map/ppermute | solution.py:20
  50.3 2.2 %collective-permute-start.2 = (bf16[2,384,256]{2,1,0:T(8,128)(2,1)}, bf16[2,384,256]{2,1,0:T(8,128)(2,1)}, u32[]{:S(2)}, u32[]{:S(2)}) collective-permute-start(bf16[2,384,256]{2,1,0:T(8,128)(2,1)} %get-tuple-element.20), channel_id=1, source_target_pairs={{0,64},{32,96},{64,0},{96,32},{128,192},{160,224},{192,128},{224,1... | collective-permute-start | bytes 1179656 | tf_op jit(solution)/shard_map/ppermute | solution.py:20
  52.4 3.1 %collective-permute-start.1 = (bf16[2,384,256]{2,1,0:T(8,128)(2,1)}, bf16[2,384,256]{2,1,0:T(8,128)(2,1)}, u32[]{:S(2)}, u32[]{:S(2)}) collective-permute-start(bf16[2,384,256]{2,1,0:T(8,128)(2,1)} %get-tuple-element.7), channel_id=1, source_target_pairs={{0,32},{32,0},{64,96},{96,64},{128,160},{160,128},{192,224},{224,1... | collective-permute-start | bytes 1179656 | tf_op jit(solution)/shard_map/ppermute | solution.py:20
  57.1 4.0 %collective-permute-start = (bf16[384,256]{1,0:T(8,128)(2,1)S(1)}, bf16[384,256]{1,0:T(8,128)(2,1)S(1)}, u32[]{:S(2)}, u32[]{:S(2)}) collective-permute-start(bf16[384,256]{1,0:T(8,128)(2,1)S(1)} %bitcast.209), channel_id=1, source_target_pairs={{1,0},{2,1},{3,2},{4,3},{5,4},{6,5},{7,6},{8,7},{9,8},{10,9},{11,1... | collective-permute-start | bytes 589832 | tf_op jit(solution)/shard_map/ppermute | solution.py:16
  61.0 27.2 %collective-permute-done.4 = bf16[2,384,256]{2,1,0:T(8,128)(2,1)} collective-permute-done((bf16[2,384,256]{2,1,0:T(8,128)(2,1)}, bf16[2,384,256]{2,1,0:T(8,128)(2,1)}, u32[]{:S(2)}, u32[]{:S(2)}) %collective-permute-start.4) | collective-permute-done | bytes 393248 | tf_op jit(solution)/shard_map/ppermute | solution.py:20
  88.3 2.9 %collective-permute-start.6 = (bf16[384,256]{1,0:T(8,128)(2,1)S(1)}, bf16[384,256]{1,0:T(8,128)(2,1)S(1)}, u32[]{:S(2)}, u32[]{:S(2)}) collective-permute-start(bf16[384,256]{1,0:T(8,128)(2,1)S(1)} %convolution_convert_fusion.3), channel_id=1, source_target_pairs={{0,1},{1,2},{2,3},{3,4},{4,5},{5,6},{6,7},{7,8},{8,9},{9,10},{10,1... | collective-permute-start | bytes 589832 | tf_op jit(solution)/shard_map/ppermute | solution.py:16
  91.2 13.1 %collective-permute-done.3 = bf16[2,384,256]{2,1,0:T(8,128)(2,1)} collective-permute-done((bf16[2,384,256]{2,1,0:T(8,128)(2,1)}, bf16[2,384,256]{2,1,0:T(8,128)(2,1)}, u32[]{:S(2)}, u32[]{:S(2)}) %collective-permute-start.3) | collective-permute-done | bytes 393248 | tf_op jit(solution)/shard_map/ppermute | solution.py:20
  104.3 15.5 %collective-permute-done.1 = bf16[2,384,256]{2,1,0:T(8,128)(2,1)} collective-permute-done((bf16[2,384,256]{2,1,0:T(8,128)(2,1)}, bf16[2,384,256]{2,1,0:T(8,128)(2,1)}, u32[]{:S(2)}, u32[]{:S(2)}) %collective-permute-start.1) | collective-permute-done | bytes 393248 | tf_op jit(solution)/shard_map/ppermute | solution.py:20
  119.8 1.6 add_bitcast_fusion.12
  121.4 1.6 add_bitcast_fusion.11
  125.8 2.1 %collective-permute-start.12 = (bf16[2,384,256]{2,1,0:T(8,128)(2,1)S(1)}, bf16[2,384,256]{2,1,0:T(8,128)(2,1)S(1)}, u32[]{:S(2)}, u32[]{:S(2)}) collective-permute-start(bf16[2,384,256]{2,1,0:T(8,128)(2,1)S(1)} %add_bitcast_fusion.4), channel_id=1, source_target_pairs={{0,512},{32,544},{64,576},{96,608},{128,640},{160,672},{192,704},{... | collective-permute-start | bytes 1179656 | tf_op jit(solution)/shard_map/ppermute | solution.py:20
  127.9 4.1 %collective-permute-start.11 = (bf16[2,384,256]{2,1,0:T(8,128)(2,1)S(1)}, bf16[2,384,256]{2,1,0:T(8,128)(2,1)S(1)}, u32[]{:S(2)}, u32[]{:S(2)}) collective-permute-start(bf16[2,384,256]{2,1,0:T(8,128)(2,1)S(1)} %get-tuple-element.15), channel_id=1, source_target_pairs={{0,256},{32,288},{64,320},{96,352},{128,384},{160,416},{192,448},{... | collective-permute-start | bytes 1179656 | tf_op jit(solution)/shard_map/ppermute | solution.py:20
  132.0 1.9 collective-permute-start.10
  133.9 6.3 %collective-permute-start.9 = (bf16[2,384,256]{2,1,0:T(8,128)(2,1)S(1)}, bf16[2,384,256]{2,1,0:T(8,128)(2,1)S(1)}, u32[]{:S(2)}, u32[]{:S(2)}) collective-permute-start(bf16[2,384,256]{2,1,0:T(8,128)(2,1)S(1)} %get-tuple-element.13), channel_id=1, source_target_pairs={{0,64},{32,96},{64,0},{96,32},{128,192},{160,224},{192,128},{224,1... | collective-permute-start | bytes 1179656 | tf_op jit(solution)/shard_map/ppermute | solution.py:20
  140.2 1.9 collective-permute-start.8
  142.7 6.2 %collective-permute-start.7 = (bf16[384,256]{1,0:T(8,128)(2,1)S(1)}, bf16[384,256]{1,0:T(8,128)(2,1)S(1)}, u32[]{:S(2)}, u32[]{:S(2)}) collective-permute-start(bf16[384,256]{1,0:T(8,128)(2,1)S(1)} %fusion.17), channel_id=1, source_target_pairs={{1,0},{2,1},{3,2},{4,3},{5,4},{6,5},{7,6},{8,7},{9,8},{10,9},{11,1... | collective-permute-start | bytes 589832 | tf_op jit(solution)/shard_map/ppermute | solution.py:16
  148.8 27.5 %collective-permute-done.11 = bf16[2,384,256]{2,1,0:T(8,128)(2,1)S(1)} collective-permute-done((bf16[2,384,256]{2,1,0:T(8,128)(2,1)S(1)}, bf16[2,384,256]{2,1,0:T(8,128)(2,1)S(1)}, u32[]{:S(2)}, u32[]{:S(2)}) %collective-permute-start.11) | collective-permute-done | bytes 393248 | tf_op jit(solution)/shard_map/ppermute | solution.py:20
  176.4 3.7 %collective-permute-start.13 = (bf16[384,256]{1,0:T(8,128)(2,1)S(1)}, bf16[384,256]{1,0:T(8,128)(2,1)S(1)}, u32[]{:S(2)}, u32[]{:S(2)}) collective-permute-start(bf16[384,256]{1,0:T(8,128)(2,1)S(1)} %convolution_convert_fusion.2), channel_id=1, source_target_pairs={{0,1},{1,2},{2,3},{3,4},{4,5},{5,6},{6,7},{7,8},{8,9},{9,10},{10,1... | collective-permute-start | bytes 589832 | tf_op jit(solution)/shard_map/ppermute | solution.py:16
  180.0 9.7 %collective-permute-done.10 = bf16[2,384,256]{2,1,0:T(8,128)(2,1)S(1)} collective-permute-done((bf16[2,384,256]{2,1,0:T(8,128)(2,1)S(1)}, bf16[2,384,256]{2,1,0:T(8,128)(2,1)S(1)}, u32[]{:S(2)}, u32[]{:S(2)}) %collective-permute-start.10) | collective-permute-done | bytes 393248 | tf_op jit(solution)/shard_map/ppermute | solution.py:20
  189.7 16.7 %collective-permute-done.8 = bf16[2,384,256]{2,1,0:T(8,128)(2,1)S(1)} collective-permute-done((bf16[2,384,256]{2,1,0:T(8,128)(2,1)S(1)}, bf16[2,384,256]{2,1,0:T(8,128)(2,1)S(1)}, u32[]{:S(2)}, u32[]{:S(2)}) %collective-permute-start.8) | collective-permute-done | bytes 393248 | tf_op jit(solution)/shard_map/ppermute | solution.py:20
  (59 shorter events, 11.2 us)
Async XLA Ops:
  0.0 56.5 %copy-start = (bf16[1,1,384,384]{3,2,1,0:T(8,128)(2,1)S(1)}, bf16[1,1,384,384]{3,2,1,0:T(8,128)(2,1)}, u32[]{:S(2)}) copy-start(bf16[1,1,384,384]{3,2,1,0:T(8,128)(2,1)} %param.8) | copy-start | bytes 884740
  0.0 8.1 %copy-start.3 = (s32[1,1,4,3,3]{2,1,4,3,0:T(1,128)S(1)}, s32[1,1,4,3,3]{2,1,4,3,0:T(1,128)}, u32[]{:S(2)}) copy-start(s32[1,1,4,3,3]{2,1,4,3,0:T(1,128)} %param.10) | copy-start | bytes 436
  6.3 2.2 %copy-start.1 = (bf16[1,1,384,256]{3,2,1,0:T(8,128)(2,1)S(1)}, bf16[1,1,384,256]{3,2,1,0:T(8,128)(2,1)}, u32[]{:S(2)}) copy-start(bf16[1,1,384,256]{3,2,1,0:T(8,128)(2,1)} %param.7) | copy-start | bytes 589828
  10.9 46.2 %collective-permute-start.5 = (bf16[2,384,256]{2,1,0:T(8,128)(2,1)}, bf16[2,384,256]{2,1,0:T(8,128)(2,1)S(1)}, u32[]{:S(2)}, u32[]{:S(2)}) collective-permute-start(bf16[2,384,256]{2,1,0:T(8,128)(2,1)} %fusion.29), channel_id=1, source_target_pairs={{0,512},{32,544},{64,576},{96,608},{128,640},{160,672},{192,704},{... | collective-permute-start | bytes 1179656 | tf_op jit(solution)/shard_map/ppermute | solution.py:20
  27.0 28.7 %copy-start.2 = (bf16[1,1,384,384]{3,2,1,0:T(8,128)(2,1)S(1)}, bf16[1,1,384,384]{3,2,1,0:T(8,128)(2,1)}, u32[]{:S(2)}) copy-start(bf16[1,1,384,384]{3,2,1,0:T(8,128)(2,1)} %param.11) | copy-start | bytes 884740
  27.0 28.9 %copy-start.4 = (s32[1,1,3,3]{3,1,2,0:T(1,128)S(1)}, s32[1,1,3,3]{3,1,2,0:T(1,128)}, u32[]{:S(2)}) copy-start(s32[1,1,3,3]{3,1,2,0:T(1,128)} %param.12) | copy-start | bytes 112
  27.0 61.3 %collective-permute-start.4 = (bf16[2,384,256]{2,1,0:T(8,128)(2,1)}, bf16[2,384,256]{2,1,0:T(8,128)(2,1)}, u32[]{:S(2)}, u32[]{:S(2)}) collective-permute-start(bf16[2,384,256]{2,1,0:T(8,128)(2,1)} %get-tuple-element.22), channel_id=1, source_target_pairs={{0,256},{32,288},{64,320},{96,352},{128,384},{160,416},{192,448},{... | collective-permute-start | bytes 1179656 | tf_op jit(solution)/shard_map/ppermute | solution.py:20
  44.4 59.9 %collective-permute-start.3 = (bf16[2,384,256]{2,1,0:T(8,128)(2,1)}, bf16[2,384,256]{2,1,0:T(8,128)(2,1)}, u32[]{:S(2)}, u32[]{:S(2)}) collective-permute-start(bf16[2,384,256]{2,1,0:T(8,128)(2,1)} %get-tuple-element.21), channel_id=1, source_target_pairs={{0,128},{32,160},{64,192},{96,224},{128,0},{160,32},{192,64},{224,... | collective-permute-start | bytes 1179656 | tf_op jit(solution)/shard_map/ppermute | solution.py:20
  50.3 54.0 %collective-permute-start.2 = (bf16[2,384,256]{2,1,0:T(8,128)(2,1)}, bf16[2,384,256]{2,1,0:T(8,128)(2,1)}, u32[]{:S(2)}, u32[]{:S(2)}) collective-permute-start(bf16[2,384,256]{2,1,0:T(8,128)(2,1)} %get-tuple-element.20), channel_id=1, source_target_pairs={{0,64},{32,96},{64,0},{96,32},{128,192},{160,224},{192,128},{224,1... | collective-permute-start | bytes 1179656 | tf_op jit(solution)/shard_map/ppermute | solution.py:20
  52.4 67.3 %collective-permute-start.1 = (bf16[2,384,256]{2,1,0:T(8,128)(2,1)}, bf16[2,384,256]{2,1,0:T(8,128)(2,1)}, u32[]{:S(2)}, u32[]{:S(2)}) collective-permute-start(bf16[2,384,256]{2,1,0:T(8,128)(2,1)} %get-tuple-element.7), channel_id=1, source_target_pairs={{0,32},{32,0},{64,96},{96,64},{128,160},{160,128},{192,224},{224,1... | collective-permute-start | bytes 1179656 | tf_op jit(solution)/shard_map/ppermute | solution.py:20
  57.1 66.7 %collective-permute-start = (bf16[384,256]{1,0:T(8,128)(2,1)S(1)}, bf16[384,256]{1,0:T(8,128)(2,1)S(1)}, u32[]{:S(2)}, u32[]{:S(2)}) collective-permute-start(bf16[384,256]{1,0:T(8,128)(2,1)S(1)} %bitcast.209), channel_id=1, source_target_pairs={{1,0},{2,1},{3,2},{4,3},{5,4},{6,5},{7,6},{8,7},{9,8},{10,9},{11,1... | collective-permute-start | bytes 589832 | tf_op jit(solution)/shard_map/ppermute | solution.py:16
  88.3 35.5 %collective-permute-start.6 = (bf16[384,256]{1,0:T(8,128)(2,1)S(1)}, bf16[384,256]{1,0:T(8,128)(2,1)S(1)}, u32[]{:S(2)}, u32[]{:S(2)}) collective-permute-start(bf16[384,256]{1,0:T(8,128)(2,1)S(1)} %convolution_convert_fusion.3), channel_id=1, source_target_pairs={{0,1},{1,2},{2,3},{3,4},{4,5},{5,6},{6,7},{7,8},{8,9},{9,10},{10,1... | collective-permute-start | bytes 589832 | tf_op jit(solution)/shard_map/ppermute | solution.py:16
  125.8 16.8 %collective-permute-start.12 = (bf16[2,384,256]{2,1,0:T(8,128)(2,1)S(1)}, bf16[2,384,256]{2,1,0:T(8,128)(2,1)S(1)}, u32[]{:S(2)}, u32[]{:S(2)}) collective-permute-start(bf16[2,384,256]{2,1,0:T(8,128)(2,1)S(1)} %add_bitcast_fusion.4), channel_id=1, source_target_pairs={{0,512},{32,544},{64,576},{96,608},{128,640},{160,672},{192,704},{... | collective-permute-start | bytes 1179656 | tf_op jit(solution)/shard_map/ppermute | solution.py:20
  127.9 48.5 %collective-permute-start.11 = (bf16[2,384,256]{2,1,0:T(8,128)(2,1)S(1)}, bf16[2,384,256]{2,1,0:T(8,128)(2,1)S(1)}, u32[]{:S(2)}, u32[]{:S(2)}) collective-permute-start(bf16[2,384,256]{2,1,0:T(8,128)(2,1)S(1)} %get-tuple-element.15), channel_id=1, source_target_pairs={{0,256},{32,288},{64,320},{96,352},{128,384},{160,416},{192,448},{... | collective-permute-start | bytes 1179656 | tf_op jit(solution)/shard_map/ppermute | solution.py:20
  132.0 57.8 %collective-permute-start.10 = (bf16[2,384,256]{2,1,0:T(8,128)(2,1)S(1)}, bf16[2,384,256]{2,1,0:T(8,128)(2,1)S(1)}, u32[]{:S(2)}, u32[]{:S(2)}) collective-permute-start(bf16[2,384,256]{2,1,0:T(8,128)(2,1)S(1)} %get-tuple-element.14), channel_id=1, source_target_pairs={{0,128},{32,160},{64,192},{96,224},{128,0},{160,32},{192,64},{224,... | collective-permute-start | bytes 1179656 | tf_op jit(solution)/shard_map/ppermute | solution.py:20
  133.9 55.8 %collective-permute-start.9 = (bf16[2,384,256]{2,1,0:T(8,128)(2,1)S(1)}, bf16[2,384,256]{2,1,0:T(8,128)(2,1)S(1)}, u32[]{:S(2)}, u32[]{:S(2)}) collective-permute-start(bf16[2,384,256]{2,1,0:T(8,128)(2,1)S(1)} %get-tuple-element.13), channel_id=1, source_target_pairs={{0,64},{32,96},{64,0},{96,32},{128,192},{160,224},{192,128},{224,1... | collective-permute-start | bytes 1179656 | tf_op jit(solution)/shard_map/ppermute | solution.py:20
  140.2 66.3 %collective-permute-start.8 = (bf16[2,384,256]{2,1,0:T(8,128)(2,1)S(1)}, bf16[2,384,256]{2,1,0:T(8,128)(2,1)S(1)}, u32[]{:S(2)}, u32[]{:S(2)}) collective-permute-start(bf16[2,384,256]{2,1,0:T(8,128)(2,1)S(1)} %get-tuple-element.5), channel_id=1, source_target_pairs={{0,32},{32,0},{64,96},{96,64},{128,160},{160,128},{192,224},{224,1... | collective-permute-start | bytes 1179656 | tf_op jit(solution)/shard_map/ppermute | solution.py:20
  142.7 65.2 %collective-permute-start.7 = (bf16[384,256]{1,0:T(8,128)(2,1)S(1)}, bf16[384,256]{1,0:T(8,128)(2,1)S(1)}, u32[]{:S(2)}, u32[]{:S(2)}) collective-permute-start(bf16[384,256]{1,0:T(8,128)(2,1)S(1)} %fusion.17), channel_id=1, source_target_pairs={{1,0},{2,1},{3,2},{4,3},{5,4},{6,5},{7,6},{8,7},{9,8},{10,9},{11,1... | collective-permute-start | bytes 589832 | tf_op jit(solution)/shard_map/ppermute | solution.py:16
  176.4 31.5 %collective-permute-start.13 = (bf16[384,256]{1,0:T(8,128)(2,1)S(1)}, bf16[384,256]{1,0:T(8,128)(2,1)S(1)}, u32[]{:S(2)}, u32[]{:S(2)}) collective-permute-start(bf16[384,256]{1,0:T(8,128)(2,1)S(1)} %convolution_convert_fusion.2), channel_id=1, source_target_pairs={{0,1},{1,2},{2,3},{3,4},{4,5},{5,6},{6,7},{7,8},{8,9},{9,10},{10,1... | collective-permute-start | bytes 589832 | tf_op jit(solution)/shard_map/ppermute | solution.py:16
where the time goes:
time: 210 us; the launch traced here: 209 us
  waiting for transfers between devices  110 us (52%)
  starting transfers between devices  69 us (33%)
  between operations  12.8 us (6%)
  other arithmetic  9 us (4%)
  matrix products  5.18 us (2%)
  local copies, waits for them, and re-layouts  3.19 us (2%)
    ppermute x10, waiting for transfers between devices, from_partner(): lax.ppermute(x, axis, [(i, i ^ 1 << distance) for i in range(lax.axis_siz...  110 us
    ppermute x10, starting transfers between devices, from_partner(): lax.ppermute(x, axis, [(i, i ^ 1 << distance) for i in range(lax.axis_siz...  52.2 us
    ppermute x4, starting transfers between devices, from_behind(): return lax.ppermute(block, axis, route)  16.8 us
  transfers between devices with their start and end apart: 14, of which 6 were waited for; matrix products, arithmetic and copies ran while one was open for 4% of the time, Pallas kernels for 0%

commit v1 on v0

v1 whole, which is shorter than its diff:
```python
import jax
import jax.numpy as jnp
from jax import lax
from jax.experimental import pallas as pl
from jax.experimental.pallas import tpu as pltpu
from jax.sharding import PartitionSpec as P

BLK = 128
RB = 3
R = 384
NV = 256
MATCH = 4
BITS = 5

spectrum_center = 1.0
spectrum_halfwidth = 6.0

VMEM = pl.BlockSpec(memory_space=pltpu.VMEM)
SMEM = pl.BlockSpec(memory_space=pltpu.SMEM)

ROWS = jax.ShapeDtypeStruct((R, NV), jnp.bfloat16)
PAIR = jax.ShapeDtypeStruct((2, R, NV), jnp.bfloat16)
TOTAL = jax.ShapeDtypeStruct((R, NV), jnp.float32)


def dot(a, b):
    return jnp.dot(a, b, preferred_element_type=jnp.float32)


def product(block, rows):
    return dot(block, rows).astype(jnp.bfloat16)


def masked(block, mask):
    return block * jnp.full((BLK, BLK), mask.astype(jnp.float32)).astype(jnp.bfloat16)


def prepare(group, matchings, pair_masks, shell_mask, v, pair, shell, local,
            pb, pt, cb, ct, lt, q3, q2, s1, s0, s4, up, total):
    g = group[0]
    rows = v[...]
    for b in (3, 2, 1, 0, 4):
        place, present = jnp.int32(0), jnp.int32(0)
        for m in range(MATCH):
            hit = (jnp.bitwise_xor(matchings[m, g], g) == 1 << b).astype(jnp.int32)
            place, present = place + hit * m, present + hit
        for i in range(RB):
            for j in range(RB):
                block = pair[place, i * BLK:(i + 1) * BLK, j * BLK:(j + 1) * BLK]
                block = masked(block, pair_masks[place * RB * RB + i * RB + j] * present)
                pb[b, i * BLK:(i + 1) * BLK, j * BLK:(j + 1) * BLK] = block
                pt[b, j * BLK:(j + 1) * BLK, i * BLK:(i + 1) * BLK] = block.T
        q = product(pt[b], rows)
        if b == 3:
            q3[...] = q
        elif b == 2:
            q2[...] = q
        else:
            send = {0: s0, 1: s1, 4: s4}[b]
            send[0] = rows
            send[1] = q
    for i in range(RB):
        for j in range(RB):
            block = masked(shell[i * BLK:(i + 1) * BLK, j * BLK:(j + 1) * BLK], shell_mask[i * RB + j])
            cb[i * BLK:(i + 1) * BLK, j * BLK:(j + 1) * BLK] = block
            ct[j * BLK:(j + 1) * BLK, i * BLK:(i + 1) * BLK] = block.T
    up[...] = product(ct[...], rows)
    lt[...] = local[...].T
    total[...] = dot(local[...], rows) + dot(lt[...], rows) - spectrum_center * rows.astype(jnp.float32)


def spread(v, pt, local, lt, ct, q2, s1, s0, s4, up, total):
    rows = v[...]
    q2[...] = product(pt[2], rows)
    for b, send in ((1, s1), (0, s0), (4, s4)):
        send[0] = rows
        send[1] = product(pt[b], rows)
    up[...] = product(ct[...], rows)
    total[...] = dot(local[...], rows) + dot(lt[...], rows) - spectrum_center * rows.astype(jnp.float32)


def collected(total, v2, v3, q, r1, r0, r4, higher, lower, pb, cb):
    image = total[...] + dot(pb[2], v2[...]) + dot(pb[3], v3[...]) + dot(cb[...], higher[...])
    for b, r in ((1, r1), (0, r0), (4, r4)):
        image = image + dot(pb[b], r[0]) + r[1].astype(jnp.float32)
    return image + q[...].astype(jnp.float32) + lower[...].astype(jnp.float32)


def first(total, v2, v3, q, r1, r0, r4, higher, lower, pb, cb, pt, out, q3):
    image = collected(total, v2, v3, q, r1, r0, r4, higher, lower, pb, cb)
    rows = (image / spectrum_halfwidth).astype(jnp.bfloat16)
    out[...] = rows
    q3[...] = product(pt[3], rows)


def second(total, v2, v3, q, r1, r0, r4, higher, lower, pb, cb, v, out):
    image = collected(total, v2, v3, q, r1, r0, r4, higher, lower, pb, cb)
    out[...] = (2.0 * image / spectrum_halfwidth - v[...].astype(jnp.float32)).astype(jnp.bfloat16)


def flops(products):
    return pl.CostEstimate(flops=products * 2 * R * R * NV, bytes_accessed=4 * R * R, transcendentals=0)


def call(body, outs, n_smem, n_vmem, products):
    return pl.pallas_call(
        body,
        out_shape=outs,
        in_specs=[SMEM] * n_smem + [VMEM] * n_vmem,
        out_specs=jax.tree.map(lambda _: VMEM, outs),
        cost_estimate=flops(products),
    )


def from_behind(block, distance):
    size = lax.axis_size("shell")
    return lax.ppermute(block, "shell", [(i - distance, i) for i in range(size) if 0 <= i - distance < size])


def from_partner(x, flip):
    return lax.ppermute(x, "grp", [(i, i ^ flip) for i in range(lax.axis_size("grp"))])


def exchange(v, q3, q2, s1, s0, s4, up):
    v2 = from_partner(v, 4)
    q3 = from_partner(q3, 12)
    r0 = from_partner(s0, 1)
    r1 = from_partner(s1, 2)
    r4 = from_partner(s4, 16)
    higher = from_behind(v, -1)
    lower = from_behind(up, 1)
    v3 = from_partner(v2, 12)
    q = from_partner((q2.astype(jnp.float32) + q3.astype(jnp.float32)).astype(jnp.bfloat16), 4)
    return v2, v3, q, r1, r0, r4, higher, lower


def on_device(vectors, local_block, pair_blocks, pair_masks, shell_block, shell_mask, matchings):
    v = vectors[0, 0]
    local = local_block[0, 0]
    group = lax.axis_index("grp").astype(jnp.int32).reshape(1)
    square = jax.ShapeDtypeStruct((R, R), jnp.bfloat16)
    stack = jax.ShapeDtypeStruct((BITS, R, R), jnp.bfloat16)
    pb, pt, cb, ct, lt, q3, q2, s1, s0, s4, up, total = call(
        prepare, [stack, stack, square, square, square, ROWS, ROWS, PAIR, PAIR, PAIR, ROWS, TOTAL], 4, 4, 8
    )(group, matchings, pair_masks.reshape(-1), shell_mask.reshape(-1), v, pair_blocks[0, 0], shell_block[0, 0], local)
    parts = exchange(v, q3, q2, s1, s0, s4, up)
    w, q3 = call(first, [ROWS, ROWS], 0, 12, 7)(total, *parts, pb, cb, pt)
    q2, s1, s0, s4, up, total = call(spread, [ROWS, PAIR, PAIR, PAIR, ROWS, TOTAL], 0, 5, 7)(w, pt, local, lt, ct)
    parts = exchange(w, q3, q2, s1, s0, s4, up)
    out = call(second, ROWS, 0, 12, 6)(total, *parts, pb, cb, v)
    return out[None, None]


def solution(mesh):
    in_specs = (
        P("grp", "shell", None, None),
        P("grp", "shell", None, None),
        P("grp", "shell", None, None, None),
        P("grp", "shell", None, None, None),
        P("grp", "shell", None, None),
        P("grp", "shell", None, None),
        P(),
    )
    out_specs = P("grp", "shell", None, None)
    return jax.shard_map(
        on_device, mesh=mesh, in_specs=in_specs, out_specs=out_specs, check_vma=False
    )
```

time: 210 us -> 165 us (0.79)
  the two profiles are of different devices: /device:TPU:129 before, /device:TPU:55 now
where the time goes in v1:
time: 165 us; the launch traced here: 164 us
  starting transfers between devices  93.7 us (57%)
  waiting for transfers between devices  47.9 us (29%)
  Pallas kernels  16.5 us (10%)
  local copies, waits for them, and re-layouts  3.32 us (2%)
  other arithmetic  2.66 us (2%)
    ppermute x14, starting transfers between devices, from_partner(): lax.ppermute(x, 'grp', [(i, i ^ flip) for i in range(lax.axis_size('grp'))])  84.8 us
    ppermute x14, waiting for transfers between devices, from_partner(): lax.ppermute(x, 'grp', [(i, i ^ flip) for i in range(lax.axis_size('grp'))])  47.9 us
    ppermute x4, starting transfers between devices, from_behind(): lax.ppermute(block, 'shell', [(i - distance, i) for i in range(size) if 0...  8.9 us
    pallas_call x1, Pallas kernels, on_device(): w, q3 = call(first, [ROWS, ROWS], 0, 12, 7)(total, *parts, pb, cb, pt)  4.7 us
    pallas_call x1, Pallas kernels, on_device(): call(prepare, [stack, stack, square, square, square, ROWS, ROWS, PAIR, PA...  4.66 us
    pallas_call x1, Pallas kernels, on_device(): out = call(second, ROWS, 0, 12, 6)(total, *parts, pb, cb, v)  3.82 us
    pallas_call x1, Pallas kernels, on_device(): call(spread, [ROWS, PAIR, PAIR, PAIR, ROWS, TOTAL], 0, 5, 7)  3.33 us
  transfers between devices with their start and end apart: 18, of which 5 were waited for; matrix products, arithmetic and copies ran while one was open for 1% of the time, Pallas kernels for 2%

profile of v1, /device:TPU:55, one launch (start us, length us, event | category | flops | bytes accessed | tf_op | source)
XLA Modules:
  0.0 164.5 jit_solution(3436150915147954329)
XLA Ops:
  2.7 4.7 %shard_map.73 = (bf16[5,384,384]{2,1,0:T(8,128)(2,1)}, bf16[5,384,384]{2,1,0:T(8,128)(2,1)}, bf16[384,384]{1,0:T(8,128)(2,1)}, bf16[384,384]{1,0:T(8,128)(2,1)},...) custom-call(s32[1]{0:T(128)} %bitcast.group, ...), custom_call_target="tpu_custom_call" | custom-call | flops 603979776 | bytes 589824 | tf_op jit(solution)/shard_map/pallas_call | solution.py:143
  7.4 17.9 %collective-permute-start.2 = (bf16[384,256]{1,0:T(8,128)(2,1)}, bf16[384,256]{1,0:T(8,128)(2,1)S(1)}, u32[]{:S(2)}, u32[]{:S(2)}) collective-permute-start(bf16[384,256]{1,0:T(8,128)(2,1)} %get-tuple-element.27), channel_id=1, source_target_pairs={{0,384},{32,416},{64,448},{96,480},{128,256},{160,288},{192,320},{... | collective-permute-start | bytes 589832 | tf_op jit(solution)/shard_map/ppermute | solution.py:121
  25.3 3.1 %collective-permute-start.8 = (bf16[384,256]{1,0:T(8,128)(2,1)}, bf16[384,256]{1,0:T(8,128)(2,1)S(1)}, u32[]{:S(2)}, u32[]{:S(2)}) collective-permute-start(bf16[384,256]{1,0:T(8,128)(2,1)} %get-tuple-element.31), channel_id=1, source_target_pairs={{0,1},{1,2},{2,3},{3,4},{4,5},{5,6},{6,7},{7,8},{8,9},{9,10},{10,1... | collective-permute-start | bytes 589832 | tf_op jit(solution)/shard_map/ppermute | solution.py:117
  28.4 3.4 %collective-permute-start = (bf16[384,256]{1,0:T(8,128)(2,1)S(1)}, bf16[384,256]{1,0:T(8,128)(2,1)S(1)}, u32[]{:S(2)}, u32[]{:S(2)}) collective-permute-start(bf16[384,256]{1,0:T(8,128)(2,1)S(1)} %bitcast.10), channel_id=1, source_target_pairs={{0,128},{32,160},{64,192},{96,224},{128,0},{160,32},{192,64},{224,... | collective-permute-start | bytes 589832 | tf_op jit(solution)/shard_map/ppermute | solution.py:121
  31.8 1.9 %collective-permute-start.7 = (bf16[384,256]{1,0:T(8,128)(2,1)S(1)}, bf16[384,256]{1,0:T(8,128)(2,1)S(1)}, u32[]{:S(2)}, u32[]{:S(2)}) collective-permute-start(bf16[384,256]{1,0:T(8,128)(2,1)S(1)} %bitcast.11), channel_id=1, source_target_pairs={{1,0},{2,1},{3,2},{4,3},{5,4},{6,5},{7,6},{8,7},{9,8},{10,9},{11,1... | collective-permute-start | bytes 589832 | tf_op jit(solution)/shard_map/ppermute | solution.py:117
  33.7 4.0 %collective-permute-start.4 = (bf16[2,384,256]{2,1,0:T(8,128)(2,1)}, bf16[2,384,256]{2,1,0:T(8,128)(2,1)S(1)}, u32[]{:S(2)}, u32[]{:S(2)}) collective-permute-start(bf16[2,384,256]{2,1,0:T(8,128)(2,1)} %get-tuple-element.28), channel_id=1, source_target_pairs={{0,64},{32,96},{64,0},{96,32},{128,192},{160,224},{192,128},{224,1... | collective-permute-start | bytes 1179656 | tf_op jit(solution)/shard_map/ppermute | solution.py:121
  39.5 3.7 %collective-permute-start.5 = (bf16[2,384,256]{2,1,0:T(8,128)(2,1)}, bf16[2,384,256]{2,1,0:T(8,128)(2,1)S(1)}, u32[]{:S(2)}, u32[]{:S(2)}) collective-permute-start(bf16[2,384,256]{2,1,0:T(8,128)(2,1)} %get-tuple-element.29), channel_id=1, source_target_pairs={{0,32},{32,0},{64,96},{96,64},{128,160},{160,128},{192,224},{224,1... | collective-permute-start | bytes 1179656 | tf_op jit(solution)/shard_map/ppermute | solution.py:121
  43.2 3.6 %collective-permute-start.6 = (bf16[2,384,256]{2,1,0:T(8,128)(2,1)}, bf16[2,384,256]{2,1,0:T(8,128)(2,1)S(1)}, u32[]{:S(2)}, u32[]{:S(2)}) collective-permute-start(bf16[2,384,256]{2,1,0:T(8,128)(2,1)} %get-tuple-element.30), channel_id=1, source_target_pairs={{0,512},{32,544},{64,576},{96,608},{128,640},{160,672},{192,704},{... | collective-permute-start | bytes 1179656 | tf_op jit(solution)/shard_map/ppermute | solution.py:121
  47.7 7.1 %collective-permute-start.3 = (bf16[384,256]{1,0:T(8,128)(2,1)S(1)}, bf16[384,256]{1,0:T(8,128)(2,1)S(1)}, u32[]{:S(2)}, u32[]{:S(2)}) collective-permute-start(bf16[384,256]{1,0:T(8,128)(2,1)S(1)} %add_convert_fusion.1), channel_id=1, source_target_pairs={{0,128},{32,160},{64,192},{96,224},{128,0},{160,32},{192,64},{224,... | collective-permute-start | bytes 589832 | tf_op jit(solution)/shard_map/ppermute | solution.py:121
  54.9 3.4 %collective-permute-start.1 = (bf16[384,256]{1,0:T(8,128)(2,1)S(1)}, bf16[384,256]{1,0:T(8,128)(2,1)S(1)}, u32[]{:S(2)}, u32[]{:S(2)}) collective-permute-start(bf16[384,256]{1,0:T(8,128)(2,1)S(1)} %collective-permute-done.v2), channel_id=1, source_target_pairs={{0,384},{32,416},{64,448},{96,480},{128,256},{160,288},{192,320},{... | collective-permute-start | bytes 589832 | tf_op jit(solution)/shard_map/ppermute | solution.py:121
  58.3 15.7 %collective-permute-done.3.q = bf16[384,256]{1,0:T(8,128)(2,1)S(1)} collective-permute-done((bf16[384,256]{1,0:T(8,128)(2,1)S(1)}, bf16[384,256]{1,0:T(8,128)(2,1)S(1)}, u32[]{:S(2)}, u32[]{:S(2)}) %collective-permute-start.3) | collective-permute-done | bytes 196640 | tf_op jit(solution)/shard_map/ppermute | solution.py:121
  76.2 4.7 %shard_map.74 = (bf16[384,256]{1,0:T(8,128)(2,1)}, bf16[384,256]{1,0:T(8,128)(2,1)}) custom-call(f32[384,256]{1,0:T(8,128)} %get-tuple-element.25.total, bf16[384,256]{1,0:T(8,128)(2,1)} %copy-done.10, bf16[384,256]{1,0:T(8,128)(2,1)} %copy-done.16, bf16[384,256]{1,0:T(8,128)(2,1)} %copy-done.14, bf16[2,384,256]{2,1,0:T(8,128)(2,1)} %copy-done.1, ...), custom_call_target="tpu_custom_call" | custom-call | flops 528482304 | bytes 589824 | tf_op jit(solution)/shard_map/pallas_call | solution.py:147
  80.9 8.9 %collective-permute-start.11 = (bf16[384,256]{1,0:T(8,128)(2,1)}, bf16[384,256]{1,0:T(8,128)(2,1)S(1)}, u32[]{:S(2)}, u32[]{:S(2)}) collective-permute-start(bf16[384,256]{1,0:T(8,128)(2,1)} %get-tuple-element.40), channel_id=1, source_target_pairs={{0,384},{32,416},{64,448},{96,480},{128,256},{160,288},{192,320},{... | collective-permute-start | bytes 589832 | tf_op jit(solution)/shard_map/ppermute | solution.py:121
  89.8 3.3 %shard_map.75 = (bf16[384,256]{1,0:T(8,128)(2,1)}, bf16[2,384,256]{2,1,0:T(8,128)(2,1)}, bf16[2,384,256]{2,1,0:T(8,128)(2,1)}, bf16[2,384,256]{2,1,0:T(8,128)(2,...) custom-call(bf16[384,256]{1,0:T(8,128)(2,1)} %get-tuple-element.35.v, bf16[5,384,384]{2,1,0:T(8,128)(2,1)} %get-tuple-element.34.pt, ...), custom_call_target="tpu_custom_call" | custom-call | flops 528482304 | bytes 589824 | tf_op jit(solution)/shard_map/pallas_call | solution.py:148
  95.1 5.3 %collective-permute-start.9 = (bf16[384,256]{1,0:T(8,128)(2,1)S(1)}, bf16[384,256]{1,0:T(8,128)(2,1)S(1)}, u32[]{:S(2)}, u32[]{:S(2)}) collective-permute-start(bf16[384,256]{1,0:T(8,128)(2,1)S(1)} %copy-done.17), channel_id=1, source_target_pairs={{0,128},{32,160},{64,192},{96,224},{128,0},{160,32},{192,64},{224,... | collective-permute-start | bytes 589832 | tf_op jit(solution)/shard_map/ppermute | solution.py:121
  100.4 1.9 %collective-permute-start.16 = (bf16[384,256]{1,0:T(8,128)(2,1)S(1)}, bf16[384,256]{1,0:T(8,128)(2,1)S(1)}, u32[]{:S(2)}, u32[]{:S(2)}) collective-permute-start(bf16[384,256]{1,0:T(8,128)(2,1)S(1)} %copy-done.17), channel_id=1, source_target_pairs={{1,0},{2,1},{3,2},{4,3},{5,4},{6,5},{7,6},{8,7},{9,8},{10,9},{11,1... | collective-permute-start | bytes 589832 | tf_op jit(solution)/shard_map/ppermute | solution.py:117
  102.3 10.6 %collective-permute-start.13 = (bf16[2,384,256]{2,1,0:T(8,128)(2,1)}, bf16[2,384,256]{2,1,0:T(8,128)(2,1)S(1)}, u32[]{:S(2)}, u32[]{:S(2)}) collective-permute-start(bf16[2,384,256]{2,1,0:T(8,128)(2,1)} %get-tuple-element.41), channel_id=1, source_target_pairs={{0,64},{32,96},{64,0},{96,32},{128,192},{160,224},{192,128},{224,1... | collective-permute-start | bytes 1179656 | tf_op jit(solution)/shard_map/ppermute | solution.py:121
  112.9 1.9 %collective-permute-start.14 = (bf16[2,384,256]{2,1,0:T(8,128)(2,1)}, bf16[2,384,256]{2,1,0:T(8,128)(2,1)S(1)}, u32[]{:S(2)}, u32[]{:S(2)}) collective-permute-start(bf16[2,384,256]{2,1,0:T(8,128)(2,1)} %get-tuple-element.42), channel_id=1, source_target_pairs={{0,32},{32,0},{64,96},{96,64},{128,160},{160,128},{192,224},{224,1... | collective-permute-start | bytes 1179656 | tf_op jit(solution)/shard_map/ppermute | solution.py:121
  114.9 4.4 %collective-permute-start.15 = (bf16[2,384,256]{2,1,0:T(8,128)(2,1)}, bf16[2,384,256]{2,1,0:T(8,128)(2,1)S(1)}, u32[]{:S(2)}, u32[]{:S(2)}) collective-permute-start(bf16[2,384,256]{2,1,0:T(8,128)(2,1)} %get-tuple-element.43), channel_id=1, source_target_pairs={{0,512},{32,544},{64,576},{96,608},{128,640},{160,672},{192,704},{... | collective-permute-start | bytes 1179656 | tf_op jit(solution)/shard_map/ppermute | solution.py:121
  120.3 5.1 %collective-permute-start.12 = (bf16[384,256]{1,0:T(8,128)(2,1)S(1)}, bf16[384,256]{1,0:T(8,128)(2,1)S(1)}, u32[]{:S(2)}, u32[]{:S(2)}) collective-permute-start(bf16[384,256]{1,0:T(8,128)(2,1)S(1)} %add_convert_fusion), channel_id=1, source_target_pairs={{0,128},{32,160},{64,192},{96,224},{128,0},{160,32},{192,64},{224,... | collective-permute-start | bytes 589832 | tf_op jit(solution)/shard_map/ppermute | solution.py:121
  125.4 5.4 %collective-permute-start.10 = (bf16[384,256]{1,0:T(8,128)(2,1)S(1)}, bf16[384,256]{1,0:T(8,128)(2,1)S(1)}, u32[]{:S(2)}, u32[]{:S(2)}) collective-permute-start(bf16[384,256]{1,0:T(8,128)(2,1)S(1)} %collective-permute-done.9.v2), channel_id=1, source_target_pairs={{0,384},{32,416},{64,448},{96,480},{128,256},{160,288},{192,320},{... | collective-permute-start | bytes 589832 | tf_op jit(solution)/shard_map/ppermute | solution.py:121
  130.9 15.9 %collective-permute-done.12.q = bf16[384,256]{1,0:T(8,128)(2,1)S(1)} collective-permute-done((bf16[384,256]{1,0:T(8,128)(2,1)S(1)}, bf16[384,256]{1,0:T(8,128)(2,1)S(1)}, u32[]{:S(2)}, u32[]{:S(2)}) %collective-permute-start.12) | collective-permute-done | bytes 196640 | tf_op jit(solution)/shard_map/ppermute | solution.py:121
  146.8 13.1 %collective-permute-done.10.v3 = bf16[384,256]{1,0:T(8,128)(2,1)S(1)} collective-permute-done((bf16[384,256]{1,0:T(8,128)(2,1)S(1)}, bf16[384,256]{1,0:T(8,128)(2,1)S(1)}, u32[]{:S(2)}, u32[]{:S(2)}) %collective-permute-start.10) | collective-permute-done | bytes 196640 | tf_op jit(solution)/shard_map/ppermute | solution.py:121
  160.6 3.8 %shard_map.76 = bf16[384,256]{1,0:T(8,128)(2,1)} custom-call(f32[384,256]{1,0:T(8,128)} %get-tuple-element.38.total, bf16[384,256]{1,0:T(8,128)(2,1)} %copy-done.9, bf16[384,256]{1,0:T(8,128)(2,1)} %copy-done.15, bf16[384,256]{1,0:T(8,128)(2,1)} %copy-done.13, bf16[2,384,256]{2,1,0:T(8,128)(2,1)} %copy-done, bf16[2,384,256]{2,1,0:T(8,128)(2,1)} %copy-done.2, ...), custom_call_target="tpu_custom_call" | custom-call | flops 452984832 | bytes 589824 | tf_op jit(solution)/shard_map/pallas_call | solution.py:150
  (58 shorter events, 11.1 us)
Async XLA Ops:
  0.0 28.4 %copy-start.6 = (bf16[1,1,384,256]{3,2,1,0:T(8,128)(2,1)S(1)}, bf16[1,1,384,256]{3,2,1,0:T(8,128)(2,1)}, u32[]{:S(2)}) copy-start(bf16[1,1,384,256]{3,2,1,0:T(8,128)(2,1)} %param.7) | copy-start | bytes 589828
  7.4 32.1 %collective-permute-start.2 = (bf16[384,256]{1,0:T(8,128)(2,1)}, bf16[384,256]{1,0:T(8,128)(2,1)S(1)}, u32[]{:S(2)}, u32[]{:S(2)}) collective-permute-start(bf16[384,256]{1,0:T(8,128)(2,1)} %get-tuple-element.27), channel_id=1, source_target_pairs={{0,384},{32,416},{64,448},{96,480},{128,256},{160,288},{192,320},{... | collective-permute-start | bytes 589832 | tf_op jit(solution)/shard_map/ppermute | solution.py:121
  25.3 17.9 %collective-permute-start.8 = (bf16[384,256]{1,0:T(8,128)(2,1)}, bf16[384,256]{1,0:T(8,128)(2,1)S(1)}, u32[]{:S(2)}, u32[]{:S(2)}) collective-permute-start(bf16[384,256]{1,0:T(8,128)(2,1)} %get-tuple-element.31), channel_id=1, source_target_pairs={{0,1},{1,2},{2,3},{3,4},{4,5},{5,6},{6,7},{7,8},{8,9},{9,10},{10,1... | collective-permute-start | bytes 589832 | tf_op jit(solution)/shard_map/ppermute | solution.py:117
  28.4 19.3 %collective-permute-start = (bf16[384,256]{1,0:T(8,128)(2,1)S(1)}, bf16[384,256]{1,0:T(8,128)(2,1)S(1)}, u32[]{:S(2)}, u32[]{:S(2)}) collective-permute-start(bf16[384,256]{1,0:T(8,128)(2,1)S(1)} %bitcast.10), channel_id=1, source_target_pairs={{0,128},{32,160},{64,192},{96,224},{128,0},{160,32},{192,64},{224,... | collective-permute-start | bytes 589832 | tf_op jit(solution)/shard_map/ppermute | solution.py:121
  31.8 23.1 %collective-permute-start.7 = (bf16[384,256]{1,0:T(8,128)(2,1)S(1)}, bf16[384,256]{1,0:T(8,128)(2,1)S(1)}, u32[]{:S(2)}, u32[]{:S(2)}) collective-permute-start(bf16[384,256]{1,0:T(8,128)(2,1)S(1)} %bitcast.11), channel_id=1, source_target_pairs={{1,0},{2,1},{3,2},{4,3},{5,4},{6,5},{7,6},{8,7},{9,8},{10,9},{11,1... | collective-permute-start | bytes 589832 | tf_op jit(solution)/shard_map/ppermute | solution.py:117
  33.7 40.3 %collective-permute-start.4 = (bf16[2,384,256]{2,1,0:T(8,128)(2,1)}, bf16[2,384,256]{2,1,0:T(8,128)(2,1)S(1)}, u32[]{:S(2)}, u32[]{:S(2)}) collective-permute-start(bf16[2,384,256]{2,1,0:T(8,128)(2,1)} %get-tuple-element.28), channel_id=1, source_target_pairs={{0,64},{32,96},{64,0},{96,32},{128,192},{160,224},{192,128},{224,1... | collective-permute-start | bytes 1179656 | tf_op jit(solution)/shard_map/ppermute | solution.py:121
  39.5 34.5 %collective-permute-start.5 = (bf16[2,384,256]{2,1,0:T(8,128)(2,1)}, bf16[2,384,256]{2,1,0:T(8,128)(2,1)S(1)}, u32[]{:S(2)}, u32[]{:S(2)}) collective-permute-start(bf16[2,384,256]{2,1,0:T(8,128)(2,1)} %get-tuple-element.29), channel_id=1, source_target_pairs={{0,32},{32,0},{64,96},{96,64},{128,160},{160,128},{192,224},{224,1... | collective-permute-start | bytes 1179656 | tf_op jit(solution)/shard_map/ppermute | solution.py:121
  43.2 32.4 %copy-start.8 = (bf16[384,256]{1,0:T(8,128)(2,1)}, bf16[384,256]{1,0:T(8,128)(2,1)S(1)}, u32[]{:S(2)}) copy-start(bf16[384,256]{1,0:T(8,128)(2,1)S(1)} %collective-permute-done.8.lower) | copy-start | bytes 589828
  43.2 30.9 %collective-permute-start.6 = (bf16[2,384,256]{2,1,0:T(8,128)(2,1)}, bf16[2,384,256]{2,1,0:T(8,128)(2,1)S(1)}, u32[]{:S(2)}, u32[]{:S(2)}) collective-permute-start(bf16[2,384,256]{2,1,0:T(8,128)(2,1)} %get-tuple-element.30), channel_id=1, source_target_pairs={{0,512},{32,544},{64,576},{96,608},{128,640},{160,672},{192,704},{... | collective-permute-start | bytes 1179656 | tf_op jit(solution)/shard_map/ppermute | solution.py:121
  47.7 27.8 %copy-start.10 = (bf16[384,256]{1,0:T(8,128)(2,1)}, bf16[384,256]{1,0:T(8,128)(2,1)S(1)}, u32[]{:S(2)}) copy-start(bf16[384,256]{1,0:T(8,128)(2,1)S(1)} %collective-permute-done.v2) | copy-start | bytes 589828
  47.7 26.3 %collective-permute-start.3 = (bf16[384,256]{1,0:T(8,128)(2,1)S(1)}, bf16[384,256]{1,0:T(8,128)(2,1)S(1)}, u32[]{:S(2)}, u32[]{:S(2)}) collective-permute-start(bf16[384,256]{1,0:T(8,128)(2,1)S(1)} %add_convert_fusion.1), channel_id=1, source_target_pairs={{0,128},{32,160},{64,192},{96,224},{128,0},{160,32},{192,64},{224,... | collective-permute-start | bytes 589832 | tf_op jit(solution)/shard_map/ppermute | solution.py:121
  54.9 20.6 %collective-permute-start.1 = (bf16[384,256]{1,0:T(8,128)(2,1)S(1)}, bf16[384,256]{1,0:T(8,128)(2,1)S(1)}, u32[]{:S(2)}, u32[]{:S(2)}) collective-permute-start(bf16[384,256]{1,0:T(8,128)(2,1)S(1)} %collective-permute-done.v2), channel_id=1, source_target_pairs={{0,384},{32,416},{64,448},{96,480},{128,256},{160,288},{192,320},{... | collective-permute-start | bytes 589832 | tf_op jit(solution)/shard_map/ppermute | solution.py:121
  80.9 32.1 %collective-permute-start.11 = (bf16[384,256]{1,0:T(8,128)(2,1)}, bf16[384,256]{1,0:T(8,128)(2,1)S(1)}, u32[]{:S(2)}, u32[]{:S(2)}) collective-permute-start(bf16[384,256]{1,0:T(8,128)(2,1)} %get-tuple-element.40), channel_id=1, source_target_pairs={{0,384},{32,416},{64,448},{96,480},{128,256},{160,288},{192,320},{... | collective-permute-start | bytes 589832 | tf_op jit(solution)/shard_map/ppermute | solution.py:121
  93.2 21.7 %collective-permute-start.17 = (bf16[384,256]{1,0:T(8,128)(2,1)}, bf16[384,256]{1,0:T(8,128)(2,1)S(1)}, u32[]{:S(2)}, u32[]{:S(2)}) collective-permute-start(bf16[384,256]{1,0:T(8,128)(2,1)} %get-tuple-element.44), channel_id=1, source_target_pairs={{0,1},{1,2},{2,3},{3,4},{4,5},{5,6},{6,7},{7,8},{8,9},{9,10},{10,1... | collective-permute-start | bytes 589832 | tf_op jit(solution)/shard_map/ppermute | solution.py:117
  95.1 25.2 %collective-permute-start.9 = (bf16[384,256]{1,0:T(8,128)(2,1)S(1)}, bf16[384,256]{1,0:T(8,128)(2,1)S(1)}, u32[]{:S(2)}, u32[]{:S(2)}) collective-permute-start(bf16[384,256]{1,0:T(8,128)(2,1)S(1)} %copy-done.17), channel_id=1, source_target_pairs={{0,128},{32,160},{64,192},{96,224},{128,0},{160,32},{192,64},{224,... | collective-permute-start | bytes 589832 | tf_op jit(solution)/shard_map/ppermute | solution.py:121
  100.4 25.0 %collective-permute-start.16 = (bf16[384,256]{1,0:T(8,128)(2,1)S(1)}, bf16[384,256]{1,0:T(8,128)(2,1)S(1)}, u32[]{:S(2)}, u32[]{:S(2)}) collective-permute-start(bf16[384,256]{1,0:T(8,128)(2,1)S(1)} %copy-done.17), channel_id=1, source_target_pairs={{1,0},{2,1},{3,2},{4,3},{5,4},{6,5},{7,6},{8,7},{9,8},{10,9},{11,1... | collective-permute-start | bytes 589832 | tf_op jit(solution)/shard_map/ppermute | solution.py:117
  102.3 44.4 %collective-permute-start.13 = (bf16[2,384,256]{2,1,0:T(8,128)(2,1)}, bf16[2,384,256]{2,1,0:T(8,128)(2,1)S(1)}, u32[]{:S(2)}, u32[]{:S(2)}) collective-permute-start(bf16[2,384,256]{2,1,0:T(8,128)(2,1)} %get-tuple-element.41), channel_id=1, source_target_pairs={{0,64},{32,96},{64,0},{96,32},{128,192},{160,224},{192,128},{224,1... | collective-permute-start | bytes 1179656 | tf_op jit(solution)/shard_map/ppermute | solution.py:121
  112.9 33.8 %collective-permute-start.14 = (bf16[2,384,256]{2,1,0:T(8,128)(2,1)}, bf16[2,384,256]{2,1,0:T(8,128)(2,1)S(1)}, u32[]{:S(2)}, u32[]{:S(2)}) collective-permute-start(bf16[2,384,256]{2,1,0:T(8,128)(2,1)} %get-tuple-element.42), channel_id=1, source_target_pairs={{0,32},{32,0},{64,96},{96,64},{128,160},{160,128},{192,224},{224,1... | collective-permute-start | bytes 1179656 | tf_op jit(solution)/shard_map/ppermute | solution.py:121
  114.9 45.1 %copy-start.7 = (bf16[384,256]{1,0:T(8,128)(2,1)}, bf16[384,256]{1,0:T(8,128)(2,1)S(1)}, u32[]{:S(2)}) copy-start(bf16[384,256]{1,0:T(8,128)(2,1)S(1)} %collective-permute-done.17.lower) | copy-start | bytes 589828
  114.9 31.9 %collective-permute-start.15 = (bf16[2,384,256]{2,1,0:T(8,128)(2,1)}, bf16[2,384,256]{2,1,0:T(8,128)(2,1)S(1)}, u32[]{:S(2)}, u32[]{:S(2)}) collective-permute-start(bf16[2,384,256]{2,1,0:T(8,128)(2,1)} %get-tuple-element.43), channel_id=1, source_target_pairs={{0,512},{32,544},{64,576},{96,608},{128,640},{160,672},{192,704},{... | collective-permute-start | bytes 1179656 | tf_op jit(solution)/shard_map/ppermute | solution.py:121
  120.3 39.6 %copy-start.9 = (bf16[384,256]{1,0:T(8,128)(2,1)}, bf16[384,256]{1,0:T(8,128)(2,1)S(1)}, u32[]{:S(2)}) copy-start(bf16[384,256]{1,0:T(8,128)(2,1)S(1)} %collective-permute-done.9.v2) | copy-start | bytes 589828
  120.3 26.4 %collective-permute-start.12 = (bf16[384,256]{1,0:T(8,128)(2,1)S(1)}, bf16[384,256]{1,0:T(8,128)(2,1)S(1)}, u32[]{:S(2)}, u32[]{:S(2)}) collective-permute-start(bf16[384,256]{1,0:T(8,128)(2,1)S(1)} %add_convert_fusion), channel_id=1, source_target_pairs={{0,128},{32,160},{64,192},{96,224},{128,0},{160,32},{192,64},{224,... | collective-permute-start | bytes 589832 | tf_op jit(solution)/shard_map/ppermute | solution.py:121
  125.4 34.5 %copy-start.11 = (bf16[384,256]{1,0:T(8,128)(2,1)}, bf16[384,256]{1,0:T(8,128)(2,1)S(1)}, u32[]{:S(2)}) copy-start(bf16[384,256]{1,0:T(8,128)(2,1)S(1)} %collective-permute-done.16.higher) | copy-start | bytes 589828
  125.4 34.5 %collective-permute-start.10 = (bf16[384,256]{1,0:T(8,128)(2,1)S(1)}, bf16[384,256]{1,0:T(8,128)(2,1)S(1)}, u32[]{:S(2)}, u32[]{:S(2)}) collective-permute-start(bf16[384,256]{1,0:T(8,128)(2,1)S(1)} %collective-permute-done.9.v2), channel_id=1, source_target_pairs={{0,384},{32,416},{64,448},{96,480},{128,256},{160,288},{192,320},{... | collective-permute-start | bytes 589832 | tf_op jit(solution)/shard_map/ppermute | solution.py:121
  (12 other events, 95.1 us)

commit v2 on v1

v2 whole, which is shorter than its diff:
```python
import jax
import jax.numpy as jnp
from jax import lax
from jax.experimental import pallas as pl
from jax.experimental.pallas import tpu as pltpu
from jax.sharding import PartitionSpec as P

BLK = 128
RB = 3
R = 384
NV = 256
MATCH = 4


spectrum_center = 1.0
spectrum_halfwidth = 6.0

VMEM = pl.BlockSpec(memory_space=pltpu.VMEM)
SMEM = pl.BlockSpec(memory_space=pltpu.SMEM)

ROWS = pltpu.VMEM((R, NV), jnp.bfloat16)
PAIR = pltpu.VMEM((2, R, NV), jnp.bfloat16)
TOTAL = pltpu.VMEM((R, NV), jnp.float32)
SQUARE = pltpu.VMEM((R, R), jnp.bfloat16)


def dot(a, b):
    return jnp.dot(a, b, preferred_element_type=jnp.float32)


def product(block, rows):
    return dot(block, rows).astype(jnp.bfloat16)


def wide(x):
    return x.astype(jnp.float32)


def masked(block, mask):
    return block * jnp.full((BLK, BLK), wide(mask)).astype(jnp.bfloat16)


def sorted_block(b, matchings, pair_masks, pair, pb, pt, at):
    place, present = jnp.int32(0), jnp.int32(0)
    for m in range(MATCH):
        hit = (matchings[m, 0] == 1 << b).astype(jnp.int32)
        place, present = place + hit * m, present + hit
    for i in range(RB):
        for j in range(RB):
            rows, cols = slice(i * BLK, (i + 1) * BLK), slice(j * BLK, (j + 1) * BLK)
            block = masked(pair[place, rows, cols], pair_masks[0, i, j, 0, place] * present)
            pb[at, rows, cols] = block
            pt[at, cols, rows] = block.T


def prepare_far(matchings, pair_masks, v, pair, pb, pt, q3):
    sorted_block(3, matchings, pair_masks, pair, pb, pt, 0)
    q3[...] = product(pt[0], v[...])


def prepare_near(matchings, pair_masks, shell_mask, v, pair, shell, pb, pt, ct, cb, q2, s1, s0, s4, up):
    rows = v[...]
    for at, b in enumerate((4, 1, 0, 2)):
        sorted_block(b, matchings, pair_masks, pair, pb, pt, at)
        q = product(pt[at], rows)
        if b == 2:
            q2[...] = q
        else:
            send = {0: s0, 1: s1, 4: s4}[b]
            send[0] = rows
            send[1] = q
    for i in range(RB):
        for j in range(RB):
            rs, cs = slice(i * BLK, (i + 1) * BLK), slice(j * BLK, (j + 1) * BLK)
            block = masked(shell[rs, cs], shell_mask[0, i, 0, j])
            cb[rs, cs] = block
            ct[cs, rs] = block.T
    up[...] = product(ct[...], rows)


def spread(v, pt, ct, q2, s1, s0, s4, up):
    rows = v[...]
    for at, send in ((0, s4), (1, s1), (2, s0)):
        send[0] = rows
        send[1] = product(pt[at], rows)
    q2[...] = product(pt[3], rows)
    up[...] = product(ct[...], rows)


def resident(v, local, total):
    rows = v[...]
    total[...] = dot(local[...], rows) + dot(local[...].T, rows) - spectrum_center * wide(rows)


def gathered(total, v2, r1, r0, r4, higher, lower, pb, cb, image):
    image[...] = (total[...] + dot(pb[3], v2[...]) + dot(cb[...], higher[...]) + wide(lower[...])
                  + dot(pb[1], r1[0]) + wide(r1[1]) + dot(pb[2], r0[0]) + wide(r0[1])
                  + dot(pb[0], r4[0]) + wide(r4[1]))


def first(image, v3, q, pb, pt, out, q3):
    rows = ((image[...] + wide(q[...]) + dot(pb[0], v3[...])) / spectrum_halfwidth).astype(jnp.bfloat16)
    out[...] = rows
    q3[...] = product(pt[0], rows)


def second(image, v3, q, pb, v, out):
    total = image[...] + wide(q[...]) + dot(pb[0], v3[...])
    out[...] = (2.0 * total / spectrum_halfwidth - wide(v[...])).astype(jnp.bfloat16)


def added(a, b, out):
    out[...] = (wide(a[...]) + wide(b[...])).astype(jnp.bfloat16)


def call(body, outs, products, *args, n_smem=0):
    args = args[:n_smem] + tuple(pltpu.with_memory_space_constraint(x, pltpu.VMEM) for x in args[n_smem:])
    return pl.pallas_call(
        body,
        out_shape=outs,
        in_specs=[SMEM] * n_smem + [VMEM] * (len(args) - n_smem),
        out_specs=jax.tree.map(lambda _: VMEM, outs),
        compiler_params=pltpu.CompilerParams(vmem_limit_bytes=8 << 20),
        cost_estimate=pl.CostEstimate(flops=products * 2 * R * R * NV, bytes_accessed=4 * R * R, transcendentals=0),
    )(*args)


def from_behind(block, distance):
    size = lax.axis_size("shell")
    return lax.ppermute(block, "shell", [(i - distance, i) for i in range(size) if 0 <= i - distance < size])


def from_partner(x, flip):
    return lax.ppermute(x, "grp", [(i, i ^ flip) for i in range(lax.axis_size("grp"))])


def exchange(v, q3, near, local, cb, pb):
    v2 = from_partner(v, 4)
    q3 = from_partner(q3, 12)
    q2, s1, s0, s4, up = near()
    r4 = from_partner(s4, 16)
    r1 = from_partner(s1, 2)
    r0 = from_partner(s0, 1)
    higher = from_behind(v, -1)
    lower = from_behind(up, 1)
    v3 = from_partner(v2, 12)
    q = call(added, ROWS, 1, q2, q3)
    q = from_partner(q, 4)
    total = call(resident, TOTAL, 2, v, local)
    image = call(gathered, TOTAL, 5, total, v2, r1, r0, r4, higher, lower, pb(), cb())
    return image, v3, q


def on_device(vectors, local_block, pair_blocks, pair_masks, shell_block, shell_mask, matchings):
    v = vectors[0, 0]
    local = local_block[0, 0]
    pair = pair_blocks[0, 0]
    pair_masks = jnp.transpose(pair_masks, (0, 3, 4, 1, 2))
    shell_mask = jnp.transpose(shell_mask, (0, 2, 1, 3))
    one = pltpu.VMEM((1, R, R), jnp.bfloat16)
    four = pltpu.VMEM((4, R, R), jnp.bfloat16)
    pb3, pt3, q3 = call(prepare_far, [one, one, ROWS], 3, matchings, pair_masks, v, pair, n_smem=2)
    kept = {}

    def near():
        kept["pb"], kept["pt"], kept["ct"], kept["cb"], *sends = call(
            prepare_near, [four, four, SQUARE, SQUARE, ROWS, PAIR, PAIR, PAIR, ROWS], 12,
            matchings, pair_masks, shell_mask, v, pair, shell_block[0, 0], n_smem=3)
        return sends

    parts = exchange(v, q3, near, local, lambda: kept["cb"], lambda: kept["pb"])
    w, q3 = call(first, [ROWS, ROWS], 2, *parts, pb3, pt3)
    parts = exchange(
        w, q3,
        lambda: call(spread, [ROWS, PAIR, PAIR, PAIR, ROWS], 5, w, kept["pt"], kept["ct"]),
        local, lambda: kept["cb"], lambda: kept["pb"])
    out = call(second, ROWS, 1, *parts, pb3, v)
    return out[None, None]


def solution(mesh):
    in_specs = (
        P("grp", "shell", None, None),
        P("grp", "shell", None, None),
        P("grp", "shell", None, None, None),
        P("grp", "shell", None, None, None),
        P("grp", "shell", None, None),
        P("grp", "shell", None, None),
        P(),
    )
    out_specs = P("grp", "shell", None, None)
    return jax.shard_map(
        on_device, mesh=mesh, in_specs=in_specs, out_specs=out_specs, check_vma=False
    )
```

time: 165 us -> 180 us (1.091)
  the two profiles are of different devices: /device:TPU:55 before, /device:TPU:6 now
where the time goes in v2:
time: 180 us
  starting transfers between devices  89.9 us (50%)
  waiting for transfers between devices  75.7 us (42%)
  Pallas kernels  8.78 us (5%)
  local copies, waits for them, and re-layouts  4.97 us (3%)
    ppermute x14, starting transfers between devices, from_partner(): lax.ppermute(x, 'grp', [(i, i ^ flip) for i in range(lax.axis_size('grp'))])  75.2 us
    ppermute x14, waiting for transfers between devices, from_partner(): lax.ppermute(x, 'grp', [(i, i ^ flip) for i in range(lax.axis_size('grp'))])  65.8 us
    ppermute x4, starting transfers between devices, from_behind(): lax.ppermute(block, 'shell', [(i - distance, i) for i in range(size) if 0...  14.7 us
    ppermute x4, waiting for transfers between devices, from_behind(): lax.ppermute(block, 'shell', [(i - distance, i) for i in range(size) if 0...  9.91 us
    pallas_call x11, Pallas kernels, call(): pl.pallas_call(body, out_shape=outs, in_specs=[SMEM] * n_smem + [VMEM] *...  8.78 us
    unnamed x15, local copies, waits for them, and re-layouts  4.97 us
  transfers between devices with their start and end apart: 18, of which 6 were waited for; matrix products, arithmetic and copies ran while one was open for 0% of the time, Pallas kernels for 3%

profile of v2, /device:TPU:6, one launch (start us, length us, event | category | flops | bytes accessed | tf_op | source)
XLA Modules:
  0.0 179.7 jit_solution(11622390744722026824)
XLA Ops:
  6.2 2.1 %collective-permute-start.5 = (bf16[384,256]{1,0:T(8,128)(2,1)S(1)}, bf16[384,256]{1,0:T(8,128)(2,1)S(1)}, u32[]{:S(2)}, u32[]{:S(2)}) collective-permute-start(bf16[384,256]{1,0:T(8,128)(2,1)S(1)} %get-tuple-element.27), channel_id=1, source_target_pairs={{0,1},{1,2},{2,3},{3,4},{4,5},{5,6},{6,7},{7,8},{8,9},{9,10},{10,1... | collective-permute-start | bytes 589832 | tf_op jit(solution)/shard_map/ppermute | solution.py:130
  9.5 18.2 %collective-permute-start.7 = (bf16[384,256]{1,0:T(8,128)(2,1)S(1)}, bf16[384,256]{1,0:T(8,128)(2,1)S(1)}, u32[]{:S(2)}, u32[]{:S(2)}) collective-permute-start(bf16[384,256]{1,0:T(8,128)(2,1)S(1)} %get-tuple-element.31), channel_id=1, source_target_pairs={{0,384},{32,416},{64,448},{96,480},{128,256},{160,288},{192,320},{... | collective-permute-start | bytes 589832 | tf_op jit(solution)/shard_map/ppermute | solution.py:134
  27.7 4.3 %collective-permute-start.1 = (bf16[2,384,256]{2,1,0:T(8,128)(2,1)S(1)}, bf16[2,384,256]{2,1,0:T(8,128)(2,1)S(1)}, u32[]{:S(2)}, u32[]{:S(2)}) collective-permute-start(bf16[2,384,256]{2,1,0:T(8,128)(2,1)S(1)} %get-tuple-element.24), channel_id=1, source_target_pairs={{0,64},{32,96},{64,0},{96,32},{128,192},{160,224},{192,128},{224,1... | collective-permute-start | bytes 1179656 | tf_op jit(solution)/shard_map/ppermute | solution.py:134
  32.0 3.4 %collective-permute-start.2 = (bf16[2,384,256]{2,1,0:T(8,128)(2,1)S(1)}, bf16[2,384,256]{2,1,0:T(8,128)(2,1)S(1)}, u32[]{:S(2)}, u32[]{:S(2)}) collective-permute-start(bf16[2,384,256]{2,1,0:T(8,128)(2,1)S(1)} %get-tuple-element.25), channel_id=1, source_target_pairs={{0,32},{32,0},{64,96},{96,64},{128,160},{160,128},{192,224},{224,1... | collective-permute-start | bytes 1179656 | tf_op jit(solution)/shard_map/ppermute | solution.py:134
  35.4 7.7 %collective-permute-start.3 = (bf16[2,384,256]{2,1,0:T(8,128)(2,1)S(1)}, bf16[2,384,256]{2,1,0:T(8,128)(2,1)S(1)}, u32[]{:S(2)}, u32[]{:S(2)}) collective-permute-start(bf16[2,384,256]{2,1,0:T(8,128)(2,1)S(1)} %get-tuple-element.26), channel_id=1, source_target_pairs={{0,512},{32,544},{64,576},{96,608},{128,640},{160,672},{192,704},{... | collective-permute-start | bytes 1179656 | tf_op jit(solution)/shard_map/ppermute | solution.py:134
  43.2 3.6 %collective-permute-start = (bf16[384,256]{1,0:T(8,128)(2,1)}, bf16[384,256]{1,0:T(8,128)(2,1)S(1)}, u32[]{:S(2)}, u32[]{:S(2)}) collective-permute-start(bf16[384,256]{1,0:T(8,128)(2,1)} %bitcast.v), channel_id=1, source_target_pairs={{0,128},{32,160},{64,192},{96,224},{128,0},{160,32},{192,64},{224,... | collective-permute-start | bytes 589832 | tf_op jit(solution)/shard_map/ppermute | solution.py:134
  46.8 4.9 %collective-permute-start.4 = (bf16[384,256]{1,0:T(8,128)(2,1)}, bf16[384,256]{1,0:T(8,128)(2,1)S(1)}, u32[]{:S(2)}, u32[]{:S(2)}) collective-permute-start(bf16[384,256]{1,0:T(8,128)(2,1)} %bitcast.v), channel_id=1, source_target_pairs={{1,0},{2,1},{3,2},{4,3},{5,4},{6,5},{7,6},{8,7},{9,8},{10,9},{11,1... | collective-permute-start | bytes 589832 | tf_op jit(solution)/shard_map/ppermute | solution.py:130
  51.8 14.5 %collective-permute-done.v2 = bf16[384,256]{1,0:T(8,128)(2,1)S(1)} collective-permute-done((bf16[384,256]{1,0:T(8,128)(2,1)}, bf16[384,256]{1,0:T(8,128)(2,1)S(1)}, u32[]{:S(2)}, u32[]{:S(2)}) %collective-permute-start) | collective-permute-done | bytes 196640 | tf_op jit(solution)/shard_map/ppermute | solution.py:134
  66.4 8.3 %collective-permute-start.8 = (bf16[384,256]{1,0:T(8,128)(2,1)S(1)}, bf16[384,256]{1,0:T(8,128)(2,1)S(1)}, u32[]{:S(2)}, u32[]{:S(2)}) collective-permute-start(bf16[384,256]{1,0:T(8,128)(2,1)S(1)} %shard_map.77), channel_id=1, source_target_pairs={{0,128},{32,160},{64,192},{96,224},{128,0},{160,32},{192,64},{224,... | collective-permute-start | bytes 589832 | tf_op jit(solution)/shard_map/ppermute | solution.py:134
  74.7 1.9 %collective-permute-start.6 = (bf16[384,256]{1,0:T(8,128)(2,1)S(1)}, bf16[384,256]{1,0:T(8,128)(2,1)S(1)}, u32[]{:S(2)}, u32[]{:S(2)}) collective-permute-start(bf16[384,256]{1,0:T(8,128)(2,1)S(1)} %collective-permute-done.v2), channel_id=1, source_target_pairs={{0,384},{32,416},{64,448},{96,480},{128,256},{160,288},{192,320},{... | collective-permute-start | bytes 589832 | tf_op jit(solution)/shard_map/ppermute | solution.py:134
  78.6 13.6 %collective-permute-done.8.q = bf16[384,256]{1,0:T(8,128)(2,1)S(1)} collective-permute-done((bf16[384,256]{1,0:T(8,128)(2,1)S(1)}, bf16[384,256]{1,0:T(8,128)(2,1)S(1)}, u32[]{:S(2)}, u32[]{:S(2)}) %collective-permute-start.8) | collective-permute-done | bytes 196640 | tf_op jit(solution)/shard_map/ppermute | solution.py:134
  92.2 2.3 %collective-permute-done.6.v3 = bf16[384,256]{1,0:T(8,128)(2,1)S(1)} collective-permute-done((bf16[384,256]{1,0:T(8,128)(2,1)S(1)}, bf16[384,256]{1,0:T(8,128)(2,1)S(1)}, u32[]{:S(2)}, u32[]{:S(2)}) %collective-permute-start.6) | collective-permute-done | bytes 196640 | tf_op jit(solution)/shard_map/ppermute | solution.py:134
  95.1 2.3 %collective-permute-start.16 = (bf16[384,256]{1,0:T(8,128)(2,1)S(1)}, bf16[384,256]{1,0:T(8,128)(2,1)S(1)}, u32[]{:S(2)}, u32[]{:S(2)}) collective-permute-start(bf16[384,256]{1,0:T(8,128)(2,1)S(1)} %get-tuple-element.42), channel_id=1, source_target_pairs={{0,384},{32,416},{64,448},{96,480},{128,256},{160,288},{192,320},{... | collective-permute-start | bytes 589832 | tf_op jit(solution)/shard_map/ppermute | solution.py:134
  98.1 1.9 %collective-permute-start.14 = (bf16[384,256]{1,0:T(8,128)(2,1)S(1)}, bf16[384,256]{1,0:T(8,128)(2,1)S(1)}, u32[]{:S(2)}, u32[]{:S(2)}) collective-permute-start(bf16[384,256]{1,0:T(8,128)(2,1)S(1)} %get-tuple-element.40), channel_id=1, source_target_pairs={{0,1},{1,2},{2,3},{3,4},{4,5},{5,6},{6,7},{7,8},{8,9},{9,10},{10,1... | collective-permute-start | bytes 589832 | tf_op jit(solution)/shard_map/ppermute | solution.py:130
  100.0 10.4 %collective-permute-start.10 = (bf16[2,384,256]{2,1,0:T(8,128)(2,1)S(1)}, bf16[2,384,256]{2,1,0:T(8,128)(2,1)S(1)}, u32[]{:S(2)}, u32[]{:S(2)}) collective-permute-start(bf16[2,384,256]{2,1,0:T(8,128)(2,1)S(1)} %get-tuple-element.37), channel_id=1, source_target_pairs={{0,64},{32,96},{64,0},{96,32},{128,192},{160,224},{192,128},{224,1... | collective-permute-start | bytes 1179656 | tf_op jit(solution)/shard_map/ppermute | solution.py:134
  110.4 1.9 %collective-permute-start.11 = (bf16[2,384,256]{2,1,0:T(8,128)(2,1)S(1)}, bf16[2,384,256]{2,1,0:T(8,128)(2,1)S(1)}, u32[]{:S(2)}, u32[]{:S(2)}) collective-permute-start(bf16[2,384,256]{2,1,0:T(8,128)(2,1)S(1)} %get-tuple-element.38), channel_id=1, source_target_pairs={{0,32},{32,0},{64,96},{96,64},{128,160},{160,128},{192,224},{224,1... | collective-permute-start | bytes 1179656 | tf_op jit(solution)/shard_map/ppermute | solution.py:134
  112.3 7.4 %collective-permute-start.12 = (bf16[2,384,256]{2,1,0:T(8,128)(2,1)S(1)}, bf16[2,384,256]{2,1,0:T(8,128)(2,1)S(1)}, u32[]{:S(2)}, u32[]{:S(2)}) collective-permute-start(bf16[2,384,256]{2,1,0:T(8,128)(2,1)S(1)} %get-tuple-element.39), channel_id=1, source_target_pairs={{0,512},{32,544},{64,576},{96,608},{128,640},{160,672},{192,704},{... | collective-permute-start | bytes 1179656 | tf_op jit(solution)/shard_map/ppermute | solution.py:134
  119.7 5.8 %collective-permute-start.13 = (bf16[384,256]{1,0:T(8,128)(2,1)S(1)}, bf16[384,256]{1,0:T(8,128)(2,1)S(1)}, u32[]{:S(2)}, u32[]{:S(2)}) collective-permute-start(bf16[384,256]{1,0:T(8,128)(2,1)S(1)} %get-tuple-element.34.v), channel_id=1, source_target_pairs={{1,0},{2,1},{3,2},{4,3},{5,4},{6,5},{7,6},{8,7},{9,8},{10,9},{11,1... | collective-permute-start | bytes 589832 | tf_op jit(solution)/shard_map/ppermute | solution.py:130
  125.5 1.9 %collective-permute-start.9 = (bf16[384,256]{1,0:T(8,128)(2,1)S(1)}, bf16[384,256]{1,0:T(8,128)(2,1)S(1)}, u32[]{:S(2)}, u32[]{:S(2)}) collective-permute-start(bf16[384,256]{1,0:T(8,128)(2,1)S(1)} %get-tuple-element.34.v), channel_id=1, source_target_pairs={{0,128},{32,160},{64,192},{96,224},{128,0},{160,32},{192,64},{224,... | collective-permute-start | bytes 589832 | tf_op jit(solution)/shard_map/ppermute | solution.py:134
  127.5 9.9 %collective-permute-done.13.higher = bf16[384,256]{1,0:T(8,128)(2,1)S(1)} collective-permute-done((bf16[384,256]{1,0:T(8,128)(2,1)S(1)}, bf16[384,256]{1,0:T(8,128)(2,1)S(1)}, u32[]{:S(2)}, u32[]{:S(2)}) %collective-permute-start.13) | collective-permute-done | bytes 196640 | tf_op jit(solution)/shard_map/ppermute | solution.py:130
  137.4 2.0 %collective-permute-start.17 = (bf16[384,256]{1,0:T(8,128)(2,1)S(1)}, bf16[384,256]{1,0:T(8,128)(2,1)S(1)}, u32[]{:S(2)}, u32[]{:S(2)}) collective-permute-start(bf16[384,256]{1,0:T(8,128)(2,1)S(1)} %shard_map.82), channel_id=1, source_target_pairs={{0,128},{32,160},{64,192},{96,224},{128,0},{160,32},{192,64},{224,... | collective-permute-start | bytes 589832 | tf_op jit(solution)/shard_map/ppermute | solution.py:134
  139.4 24.8 %collective-permute-done.9.v2 = bf16[384,256]{1,0:T(8,128)(2,1)S(1)} collective-permute-done((bf16[384,256]{1,0:T(8,128)(2,1)S(1)}, bf16[384,256]{1,0:T(8,128)(2,1)S(1)}, u32[]{:S(2)}, u32[]{:S(2)}) %collective-permute-start.9) | collective-permute-done | bytes 196640 | tf_op jit(solution)/shard_map/ppermute | solution.py:134
  164.1 1.9 %collective-permute-start.15 = (bf16[384,256]{1,0:T(8,128)(2,1)S(1)}, bf16[384,256]{1,0:T(8,128)(2,1)S(1)}, u32[]{:S(2)}, u32[]{:S(2)}) collective-permute-start(bf16[384,256]{1,0:T(8,128)(2,1)S(1)} %collective-permute-done.9.v2), channel_id=1, source_target_pairs={{0,384},{32,416},{64,448},{96,480},{128,256},{160,288},{192,320},{... | collective-permute-start | bytes 589832 | tf_op jit(solution)/shard_map/ppermute | solution.py:134
  167.2 10.6 %collective-permute-done.15.v3 = bf16[384,256]{1,0:T(8,128)(2,1)S(1)} collective-permute-done((bf16[384,256]{1,0:T(8,128)(2,1)S(1)}, bf16[384,256]{1,0:T(8,128)(2,1)S(1)}, u32[]{:S(2)}, u32[]{:S(2)}) %collective-permute-start.15) | collective-permute-done | bytes 196640 | tf_op jit(solution)/shard_map/ppermute | solution.py:134
  (38 shorter events, 13.8 us)
Async XLA Ops:
  0.0 1.3 copy-start.1
  1.3 0.7 copy-start.3
  2.0 0.7 copy-start.4
  2.6 1.0 copy-start.5
  4.3 3.9 %copy-start.2 = (bf16[1,1,4,384,384]{4,3,2,1,0:T(8,128)(2,1)S(1)}, bf16[1,1,4,384,384]{4,3,2,1,0:T(8,128)(2,1)}, u32[]{:S(2)}) copy-start(bf16[1,1,4,384,384]{4,3,2,1,0:T(8,128)(2,1)} %param.9) | copy-start | bytes 3538948
  6.1 70.5 %copy-start = (bf16[1,1,384,384]{3,2,1,0:T(8,128)(2,1)S(1)}, bf16[1,1,384,384]{3,2,1,0:T(8,128)(2,1)}, u32[]{:S(2)}) copy-start(bf16[1,1,384,384]{3,2,1,0:T(8,128)(2,1)} %param.8) | copy-start | bytes 884740
  6.2 37.0 %collective-permute-start.5 = (bf16[384,256]{1,0:T(8,128)(2,1)S(1)}, bf16[384,256]{1,0:T(8,128)(2,1)S(1)}, u32[]{:S(2)}, u32[]{:S(2)}) collective-permute-start(bf16[384,256]{1,0:T(8,128)(2,1)S(1)} %get-tuple-element.27), channel_id=1, source_target_pairs={{0,1},{1,2},{2,3},{3,4},{4,5},{5,6},{6,7},{7,8},{8,9},{9,10},{10,1... | collective-permute-start | bytes 589832 | tf_op jit(solution)/shard_map/ppermute | solution.py:130
  9.5 37.3 %collective-permute-start.7 = (bf16[384,256]{1,0:T(8,128)(2,1)S(1)}, bf16[384,256]{1,0:T(8,128)(2,1)S(1)}, u32[]{:S(2)}, u32[]{:S(2)}) collective-permute-start(bf16[384,256]{1,0:T(8,128)(2,1)S(1)} %get-tuple-element.31), channel_id=1, source_target_pairs={{0,384},{32,416},{64,448},{96,480},{128,256},{160,288},{192,320},{... | collective-permute-start | bytes 589832 | tf_op jit(solution)/shard_map/ppermute | solution.py:134
  27.7 50.2 %collective-permute-start.1 = (bf16[2,384,256]{2,1,0:T(8,128)(2,1)S(1)}, bf16[2,384,256]{2,1,0:T(8,128)(2,1)S(1)}, u32[]{:S(2)}, u32[]{:S(2)}) collective-permute-start(bf16[2,384,256]{2,1,0:T(8,128)(2,1)S(1)} %get-tuple-element.24), channel_id=1, source_target_pairs={{0,64},{32,96},{64,0},{96,32},{128,192},{160,224},{192,128},{224,1... | collective-permute-start | bytes 1179656 | tf_op jit(solution)/shard_map/ppermute | solution.py:134
  32.0 45.9 %collective-permute-start.2 = (bf16[2,384,256]{2,1,0:T(8,128)(2,1)S(1)}, bf16[2,384,256]{2,1,0:T(8,128)(2,1)S(1)}, u32[]{:S(2)}, u32[]{:S(2)}) collective-permute-start(bf16[2,384,256]{2,1,0:T(8,128)(2,1)S(1)} %get-tuple-element.25), channel_id=1, source_target_pairs={{0,32},{32,0},{64,96},{96,64},{128,160},{160,128},{192,224},{224,1... | collective-permute-start | bytes 1179656 | tf_op jit(solution)/shard_map/ppermute | solution.py:134
  35.4 42.5 %collective-permute-start.3 = (bf16[2,384,256]{2,1,0:T(8,128)(2,1)S(1)}, bf16[2,384,256]{2,1,0:T(8,128)(2,1)S(1)}, u32[]{:S(2)}, u32[]{:S(2)}) collective-permute-start(bf16[2,384,256]{2,1,0:T(8,128)(2,1)S(1)} %get-tuple-element.26), channel_id=1, source_target_pairs={{0,512},{32,544},{64,576},{96,608},{128,640},{160,672},{192,704},{... | collective-permute-start | bytes 1179656 | tf_op jit(solution)/shard_map/ppermute | solution.py:134
  43.2 23.2 %collective-permute-start = (bf16[384,256]{1,0:T(8,128)(2,1)}, bf16[384,256]{1,0:T(8,128)(2,1)S(1)}, u32[]{:S(2)}, u32[]{:S(2)}) collective-permute-start(bf16[384,256]{1,0:T(8,128)(2,1)} %bitcast.v), channel_id=1, source_target_pairs={{0,128},{32,160},{64,192},{96,224},{128,0},{160,32},{192,64},{224,... | collective-permute-start | bytes 589832 | tf_op jit(solution)/shard_map/ppermute | solution.py:134
  46.8 27.8 %collective-permute-start.4 = (bf16[384,256]{1,0:T(8,128)(2,1)}, bf16[384,256]{1,0:T(8,128)(2,1)S(1)}, u32[]{:S(2)}, u32[]{:S(2)}) collective-permute-start(bf16[384,256]{1,0:T(8,128)(2,1)} %bitcast.v), channel_id=1, source_target_pairs={{1,0},{2,1},{3,2},{4,3},{5,4},{6,5},{7,6},{8,7},{9,8},{10,9},{11,1... | collective-permute-start | bytes 589832 | tf_op jit(solution)/shard_map/ppermute | solution.py:130
  66.4 25.8 %collective-permute-start.8 = (bf16[384,256]{1,0:T(8,128)(2,1)S(1)}, bf16[384,256]{1,0:T(8,128)(2,1)S(1)}, u32[]{:S(2)}, u32[]{:S(2)}) collective-permute-start(bf16[384,256]{1,0:T(8,128)(2,1)S(1)} %shard_map.77), channel_id=1, source_target_pairs={{0,128},{32,160},{64,192},{96,224},{128,0},{160,32},{192,64},{224,... | collective-permute-start | bytes 589832 | tf_op jit(solution)/shard_map/ppermute | solution.py:134
  74.7 19.8 %collective-permute-start.6 = (bf16[384,256]{1,0:T(8,128)(2,1)S(1)}, bf16[384,256]{1,0:T(8,128)(2,1)S(1)}, u32[]{:S(2)}, u32[]{:S(2)}) collective-permute-start(bf16[384,256]{1,0:T(8,128)(2,1)S(1)} %collective-permute-done.v2), channel_id=1, source_target_pairs={{0,384},{32,416},{64,448},{96,480},{128,256},{160,288},{192,320},{... | collective-permute-start | bytes 589832 | tf_op jit(solution)/shard_map/ppermute | solution.py:134
  95.1 24.5 %collective-permute-start.16 = (bf16[384,256]{1,0:T(8,128)(2,1)S(1)}, bf16[384,256]{1,0:T(8,128)(2,1)S(1)}, u32[]{:S(2)}, u32[]{:S(2)}) collective-permute-start(bf16[384,256]{1,0:T(8,128)(2,1)S(1)} %get-tuple-element.42), channel_id=1, source_target_pairs={{0,384},{32,416},{64,448},{96,480},{128,256},{160,288},{192,320},{... | collective-permute-start | bytes 589832 | tf_op jit(solution)/shard_map/ppermute | solution.py:134
  98.1 27.4 %collective-permute-start.14 = (bf16[384,256]{1,0:T(8,128)(2,1)S(1)}, bf16[384,256]{1,0:T(8,128)(2,1)S(1)}, u32[]{:S(2)}, u32[]{:S(2)}) collective-permute-start(bf16[384,256]{1,0:T(8,128)(2,1)S(1)} %get-tuple-element.40), channel_id=1, source_target_pairs={{0,1},{1,2},{2,3},{3,4},{4,5},{5,6},{6,7},{7,8},{8,9},{9,10},{10,1... | collective-permute-start | bytes 589832 | tf_op jit(solution)/shard_map/ppermute | solution.py:130
  100.0 66.4 %collective-permute-start.10 = (bf16[2,384,256]{2,1,0:T(8,128)(2,1)S(1)}, bf16[2,384,256]{2,1,0:T(8,128)(2,1)S(1)}, u32[]{:S(2)}, u32[]{:S(2)}) collective-permute-start(bf16[2,384,256]{2,1,0:T(8,128)(2,1)S(1)} %get-tuple-element.37), channel_id=1, source_target_pairs={{0,64},{32,96},{64,0},{96,32},{128,192},{160,224},{192,128},{224,1... | collective-permute-start | bytes 1179656 | tf_op jit(solution)/shard_map/ppermute | solution.py:134
  110.4 56.1 %collective-permute-start.11 = (bf16[2,384,256]{2,1,0:T(8,128)(2,1)S(1)}, bf16[2,384,256]{2,1,0:T(8,128)(2,1)S(1)}, u32[]{:S(2)}, u32[]{:S(2)}) collective-permute-start(bf16[2,384,256]{2,1,0:T(8,128)(2,1)S(1)} %get-tuple-element.38), channel_id=1, source_target_pairs={{0,32},{32,0},{64,96},{96,64},{128,160},{160,128},{192,224},{224,1... | collective-permute-start | bytes 1179656 | tf_op jit(solution)/shard_map/ppermute | solution.py:134
  112.3 54.2 %collective-permute-start.12 = (bf16[2,384,256]{2,1,0:T(8,128)(2,1)S(1)}, bf16[2,384,256]{2,1,0:T(8,128)(2,1)S(1)}, u32[]{:S(2)}, u32[]{:S(2)}) collective-permute-start(bf16[2,384,256]{2,1,0:T(8,128)(2,1)S(1)} %get-tuple-element.39), channel_id=1, source_target_pairs={{0,512},{32,544},{64,576},{96,608},{128,640},{160,672},{192,704},{... | collective-permute-start | bytes 1179656 | tf_op jit(solution)/shard_map/ppermute | solution.py:134
  119.7 17.7 %collective-permute-start.13 = (bf16[384,256]{1,0:T(8,128)(2,1)S(1)}, bf16[384,256]{1,0:T(8,128)(2,1)S(1)}, u32[]{:S(2)}, u32[]{:S(2)}) collective-permute-start(bf16[384,256]{1,0:T(8,128)(2,1)S(1)} %get-tuple-element.34.v), channel_id=1, source_target_pairs={{1,0},{2,1},{3,2},{4,3},{5,4},{6,5},{7,6},{8,7},{9,8},{10,9},{11,1... | collective-permute-start | bytes 589832 | tf_op jit(solution)/shard_map/ppermute | solution.py:130
  125.5 38.7 %collective-permute-start.9 = (bf16[384,256]{1,0:T(8,128)(2,1)S(1)}, bf16[384,256]{1,0:T(8,128)(2,1)S(1)}, u32[]{:S(2)}, u32[]{:S(2)}) collective-permute-start(bf16[384,256]{1,0:T(8,128)(2,1)S(1)} %get-tuple-element.34.v), channel_id=1, source_target_pairs={{0,128},{32,160},{64,192},{96,224},{128,0},{160,32},{192,64},{224,... | collective-permute-start | bytes 589832 | tf_op jit(solution)/shard_map/ppermute | solution.py:134
  137.4 29.8 %collective-permute-start.17 = (bf16[384,256]{1,0:T(8,128)(2,1)S(1)}, bf16[384,256]{1,0:T(8,128)(2,1)S(1)}, u32[]{:S(2)}, u32[]{:S(2)}) collective-permute-start(bf16[384,256]{1,0:T(8,128)(2,1)S(1)} %shard_map.82), channel_id=1, source_target_pairs={{0,128},{32,160},{64,192},{96,224},{128,0},{160,32},{192,64},{224,... | collective-permute-start | bytes 589832 | tf_op jit(solution)/shard_map/ppermute | solution.py:134
  164.1 13.7 %collective-permute-start.15 = (bf16[384,256]{1,0:T(8,128)(2,1)S(1)}, bf16[384,256]{1,0:T(8,128)(2,1)S(1)}, u32[]{:S(2)}, u32[]{:S(2)}) collective-permute-start(bf16[384,256]{1,0:T(8,128)(2,1)S(1)} %collective-permute-done.9.v2), channel_id=1, source_target_pairs={{0,384},{32,416},{64,448},{96,480},{128,256},{160,288},{192,320},{... | collective-permute-start | bytes 589832 | tf_op jit(solution)/shard_map/ppermute | solution.py:134
  (1 other events, 0.7 us)
